TPU v7x, 8 devices: a whole 2x2x1 slice. The times are simulated.
8 devices in a mesh: ep: 4 (over z, y, x), dp: 2 (over core).
Axes of the slice: x: 2, y: 2, z: 1, core: 2. Of those that a mesh axis runs over, the one named last changes fastest.
Arguments:
- tokens: bfloat16 [4096, 256], P(('dp', 'ep'))
- dy_out: bfloat16 [4096, 256], P(('dp', 'ep'))
- dense_w1: bfloat16 [256, 256], replicated
- route_idx1: int32 [4096, 2], P(('dp', 'ep'))
- route_gate1: float32 [4096, 2], P(('dp', 'ep'))
- w_gate1: bfloat16 [8, 256, 896], P('ep')
- w_up1: bfloat16 [8, 256, 896], P('ep')
- w_down1: bfloat16 [8, 896, 256], P('ep')
- dense_w2: bfloat16 [256, 256], replicated
- route_idx2: int32 [4096, 2], P(('dp', 'ep'))
- route_gate2: float32 [4096, 2], P(('dp', 'ep'))
- w_gate2: bfloat16 [8, 256, 896], P('ep')
- w_up2: bfloat16 [8, 256, 896], P('ep')
- w_down2: bfloat16 [8, 896, 256], P('ep')
Outputs:
- output 1: bfloat16 [4096, 256], P(('dp', 'ep'))
- output 2: bfloat16 [256, 256], P(('dp', 'ep'))
- output 3: bfloat16 [8, 256, 896], P('ep', 'dp')
- output 4: bfloat16 [8, 256, 896], P('ep', 'dp')
- output 5: bfloat16 [8, 896, 256], P('ep', None, 'dp')
- output 6: bfloat16 [256, 256], P(('dp', 'ep'))
- output 7: bfloat16 [8, 256, 896], P('ep', 'dp')
- output 8: bfloat16 [8, 256, 896], P('ep', 'dp')
- output 9: bfloat16 [8, 896, 256], P('ep', None, 'dp')
All inputs are finite; a program needn't handle non-finite values.
Results may differ from a plain program's by a relative error of at most 0.02.
Values are sent between devices in bfloat16 or wider.
A program may use at most 1 GiB of HBM per device.

v0:
```python
import functools

import jax
import jax.numpy as jnp
from jax import lax
from jax.experimental import pallas as pl
from jax.experimental.pallas import tpu as pltpu
from jax.sharding import PartitionSpec as P

MESH = pl.DeviceIdType.MESH
BF = jnp.bfloat16
F32 = jnp.float32
NN = ((1,), (0,))
NT = ((1,), (1,))
TN = ((0,), (0,))
EP = 4
DP = 2
E_LOC = 2
TOK = 512
CAP = 256
D = 256
FF = 896
ROUTE, X_IN, O_ONE, DY, Y_ONE, GR_TWO, GM, GR_ONE = range(8)


def dot(a, b, dims=NN):
    return lax.dot_general(a, b, (dims, ((), ())), preferred_element_type=F32)


def place(k):
    return k + 3 * ((k + 3) // 4)


def onehot(key_row):
    rows = lax.broadcasted_iota(jnp.int32, (CAP, TOK), 0)
    return jnp.where(rows == key_row, 1.0, 0.0).astype(BF)


def gate_column(key_row, gate_row):
    rows = lax.broadcasted_iota(jnp.int32, (CAP, TOK), 0)
    return jnp.sum(jnp.where(rows == key_row, gate_row, 0.0), axis=1, keepdims=True)


def kernel(tokens, dy, route, m1, g1, u1, w1, m2, g2, u2, w2,
           dx_out, gd1, gg1, gu1, gw1, gd2, gg2, gu2, gw2,
           rt, xin, dyb, yb, gmb, oret, grt2, grt1,
           vm1, vg1, vu1, vw1, vm2, vg2, vu2, vw2,
           tri, keys, gates, keyj, x1, x2, gout, a1, b1, hb, ga, gb, u_home, p0, p1,
           wg, wu, wd, rg, ru, rd, dpart, drecv, dxb,
           loc_sem, ep_send, ep_recv, dp_send, dp_recv, all_send, all_recv, out_sem):
    me = lax.axis_index('ep')
    dp = lax.axis_index('dp')
    flat = dp * EP + me
    other = 1 - dp

    def partner(k):
        return (me // 2 + k // 2) % 2 * 2 + (me + k) % 2

    loads = [(route, rt.at[0]), (tokens, xin.at[0]), (dy, dyb.at[0]), (m1, vm1), (g1, vg1), (u1, vu1), (w1, vw1),
             (m2, vm2), (g2, vg2), (u2, vu2), (w2, vw2)]
    loads = [pltpu.make_async_copy(src, dst, loc_sem.at[n]) for n, (src, dst) in enumerate(loads)]
    for copy in loads:
        copy.start()

    barrier = pltpu.get_barrier_semaphore()
    for r in range(1, EP * DP):
        peer = (flat + r) % (EP * DP)
        pl.semaphore_signal(barrier, inc=1, device_id={'ep': peer % EP, 'dp': peer // EP}, device_id_type=MESH)
    pl.semaphore_wait(barrier, EP * DP - 1)

    def exchange(phase, k, src, dst):
        return pltpu.make_async_remote_copy(src_ref=src, dst_ref=dst, send_sem=ep_send.at[phase, k], recv_sem=ep_recv.at[phase, k],
                                            device_id={'ep': partner(k)}, device_id_type=MESH)

    def spread(phase, buf, k):
        return exchange(phase, k, buf.at[0], buf.at[k])

    def giveback(phase, buf, k):
        return exchange(phase, k, buf.at[k], buf.at[k + 3])

    loads[0].wait()
    for k in range(1, EP):
        spread(ROUTE, rt, k).start()
    loads[1].wait()
    for k in range(1, EP):
        spread(X_IN, xin, k).start()

    tri[...] = jnp.where(lax.broadcasted_iota(jnp.int32, (TOK, TOK), 0) < lax.broadcasted_iota(jnp.int32, (TOK, TOK), 1), 1.0, 0.0).astype(BF)
    expert = lax.broadcasted_iota(jnp.int32, (E_LOC * EP, TOK), 0).astype(F32)

    def make_keys(k):
        info = rt[k]
        for l in range(2):
            hit0 = info[2 * l:2 * l + 1] == expert
            hit1 = info[2 * l + 1:2 * l + 2] == expert
            both = jnp.where(hit0, 1.0, jnp.where(hit1, 1.0, 0.0))
            rank = dot(both.astype(BF), tri[...]).astype(jnp.int32)
            keys[l, k] = jnp.where(both > 0.5, rank, -1)
            gates[l, k] = jnp.where(hit0, info[4 + 2 * l:5 + 2 * l], jnp.where(hit1, info[5 + 2 * l:6 + 2 * l], 0.0))
        return info

    info = make_keys(0)
    for j in range(2):
        keyj[j] = jnp.where(info[j:j + 1] == expert, keys[0, 0], -1)
    for copy in loads[2:]:
        copy.wait()

    def mixed(x, m):
        return (x.astype(F32) + dot(x, m[...])).astype(BF)

    def forward_one(k, carry):
        @pl.when(k > 0)
        def _():
            spread(ROUTE, rt, k).wait_recv()
            make_keys(k)
            spread(X_IN, xin, k).wait_recv()

        u = mixed(xin[k], vm1)

        @pl.when(k == 0)
        def _():
            u_home[...] = u

        def one(el, c):
            rows = pl.ds(pl.multiple_of(k * CAP, CAP), CAP)
            key = keys[0, k, pl.ds(me * E_LOC + el, 1), :]
            x = dot(onehot(key), u).astype(BF)
            x1[el, rows] = x
            a = dot(x, vg1[el])
            b = dot(x, vu1[el])
            a1[el, rows] = a
            b1[el, rows] = b
            h = (a * (0.5 * jnp.tanh(0.5 * a) + 0.5) * b).astype(BF)
            oret[k, pl.ds(pl.multiple_of(el * CAP, CAP), CAP)] = dot(h, vw1[el]).astype(BF)
            return c

        lax.fori_loop(0, E_LOC, one, 0)

        @pl.when(k > 0)
        def _():
            giveback(O_ONE, oret, k).start()
        return carry

    lax.fori_loop(0, EP, forward_one, 0)
    for k in range(1, EP):
        spread(DY, dyb, k).start()

    p0[...] = jnp.zeros_like(p0)
    p1[...] = jnp.zeros_like(p1)

    def combine_one(k, carry):
        @pl.when(k > 0)
        def _():
            giveback(O_ONE, oret, k).wait_recv()

        def one(el, c):
            rows = oret[place(k), pl.ds(pl.multiple_of(el * CAP, CAP), CAP)]
            e = partner(k) * E_LOC + el
            p0[...] += dot(onehot(keyj[0, pl.ds(e, 1), :]), rows, TN)
            p1[...] += dot(onehot(keyj[1, pl.ds(e, 1), :]), rows, TN)
            return c

        lax.fori_loop(0, E_LOC, one, 0)
        return carry

    lax.fori_loop(0, EP, combine_one, 0)
    gate0 = jnp.transpose(jnp.broadcast_to(rt[0, 4:5], (8, TOK)))[:, :1]
    gate1 = jnp.transpose(jnp.broadcast_to(rt[0, 5:6], (8, TOK)))[:, :1]
    yb[0] = (u_home[...].astype(F32) + (gate0 * p0[...] + gate1 * p1[...])).astype(BF)
    for k in range(1, EP):
        spread(Y_ONE, yb, k).start()

    def expert_backward(k, el, x_rows, a, b, vg, vu, vw, ret):
        rows = pl.ds(pl.multiple_of(k * CAP, CAP), CAP)
        dh = dot(gout[el, rows], vw[el], NT).astype(BF).astype(F32)
        sig = 0.5 * jnp.tanh(0.5 * a) + 0.5
        s = a * sig
        hb[el, rows] = (s * b).astype(BF)
        grad_a = (dh * b * (sig + s * (1.0 - sig))).astype(BF)
        grad_b = (dh * s).astype(BF)
        ga[el, rows] = grad_a
        gb[el, rows] = grad_b
        back = dot(grad_a, vg[el], NT) + dot(grad_b, vu[el], NT)
        ret[k, pl.ds(pl.multiple_of(el * CAP, CAP), CAP)] = back.astype(BF)

    def layer_two(k, carry):
        @pl.when(k > 0)
        def _():
            spread(Y_ONE, yb, k).wait_recv()
            spread(DY, dyb, k).wait_recv()

        u = mixed(yb[k], vm2)

        def one(el, c):
            rows = pl.ds(pl.multiple_of(k * CAP, CAP), CAP)
            e = pl.ds(me * E_LOC + el, 1)
            key = keys[1, k, e, :]
            pick = onehot(key)
            x = dot(pick, u).astype(BF)
            x2[el, rows] = x
            gout[el, rows] = (dot(pick, dyb[k]) * gate_column(key, gates[1, k, e, :])).astype(BF)
            a = dot(x, vg2[el])
            b = dot(x, vu2[el])
            expert_backward(k, el, x, a, b, vg2, vu2, vw2, grt2)
            return c

        lax.fori_loop(0, E_LOC, one, 0)

        @pl.when(k > 0)
        def _():
            giveback(GR_TWO, grt2, k).start()
        return carry

    lax.fori_loop(0, EP, layer_two, 0)

    def pair(l, n, src, dst):
        return pltpu.make_async_remote_copy(src_ref=src, dst_ref=dst, send_sem=dp_send.at[l, n], recv_sem=dp_recv.at[l, n],
                                            device_id={'dp': other}, device_id_type=MESH)

    def pairs(l):
        return [pair(l, n, part.at[l, other], got.at[l]) for n, (part, got) in enumerate(((wg, rg), (wu, ru), (wd, rd)))]

    def weight_grads(l, x_all):
        half = D // DP

        def one(el, c):
            x = x_all[el]
            go = gout[el]
            down = dot(hb[el], go, TN).astype(BF)
            gate = dot(x, ga[el], TN).astype(BF)
            up = dot(x, gb[el], TN).astype(BF)
            for d in range(DP):
                wd[l, d, el] = down[:, d * half:(d + 1) * half]
                wg[l, d, el] = gate[d * half:(d + 1) * half]
                wu[l, d, el] = up[d * half:(d + 1) * half]
            return c

        lax.fori_loop(0, E_LOC, one, 0)
        for copy in pairs(l):
            copy.start()

    weight_grads(1, x2)

    def backward_combine(l, phase, ret, grad_y):
        p0[...] = jnp.zeros_like(p0)

        def step(k, carry):
            @pl.when(k > 0)
            def _():
                giveback(phase, ret, k).wait_recv()

            def one(el, c):
                rows = ret[place(k), pl.ds(pl.multiple_of(el * CAP, CAP), CAP)]
                e = partner(k) * E_LOC + el
                p0[...] += dot(onehot(keys[l, 0, pl.ds(e, 1), :]), rows, TN)
                return c

            lax.fori_loop(0, E_LOC, one, 0)
            return carry

        lax.fori_loop(0, EP, step, 0)
        return (grad_y.astype(F32) + p0[...]).astype(BF)

    def grad_input(grad_mixed, m):
        return (grad_mixed.astype(F32) + dot(grad_mixed, m[...], NT)).astype(BF)

    def dense_copies(l):
        copies = []
        for r in range(1, EP * DP):
            peer = (flat + r) % (EP * DP)
            copies.append(pltpu.make_async_remote_copy(
                src_ref=dpart.at[l, peer], dst_ref=drecv.at[l, r], send_sem=all_send.at[l, r], recv_sem=all_recv.at[l, r],
                device_id={'ep': peer % EP, 'dp': peer // EP}, device_id_type=MESH))
        return copies

    def dense_grad(l, x, grad_mixed):
        part = dot(x, grad_mixed, TN).astype(BF)
        for q in range(EP * DP):
            dpart[l, q] = part[q * 32:(q + 1) * 32]
        for copy in dense_copies(l):
            copy.start()

    grad_mixed = backward_combine(1, GR_TWO, grt2, dyb[0])
    gmb[0] = grad_input(grad_mixed, vm2)
    for k in range(1, EP):
        spread(GM, gmb, k).start()
    dense_grad(1, yb[0], grad_mixed)

    def backward_one(k, carry):
        @pl.when(k > 0)
        def _():
            spread(GM, gmb, k).wait_recv()

        def one(el, c):
            rows = pl.ds(pl.multiple_of(k * CAP, CAP), CAP)
            e = pl.ds(me * E_LOC + el, 1)
            key = keys[0, k, e, :]
            gout[el, rows] = (dot(onehot(key), gmb[k]) * gate_column(key, gates[0, k, e, :])).astype(BF)
            expert_backward(k, el, x1[el, rows], a1[el, rows], b1[el, rows], vg1, vu1, vw1, grt1)
            return c

        lax.fori_loop(0, E_LOC, one, 0)

        @pl.when(k > 0)
        def _():
            giveback(GR_ONE, grt1, k).start()
        return carry

    lax.fori_loop(0, EP, backward_one, 0)
    weight_grads(0, x1)

    outs = []

    def emit(src, dst):
        copy = pltpu.make_async_copy(src, dst, out_sem.at[len(outs)])
        copy.start()
        outs.append(copy)

    def finish(l, gate_out, up_out, down_out):
        for copy, part, got, out in zip(pairs(l), (wg, wu, wd), (rg, ru, rd), (gate_out, up_out, down_out)):
            copy.wait_recv()
            got[l] = (part[l, dp].astype(F32) + got[l].astype(F32)).astype(BF)
            emit(got.at[l], out)

    def finish_dense(l, out):
        total = dpart[l, flat].astype(F32)
        for r, copy in enumerate(dense_copies(l), 1):
            copy.wait_recv()
            total += drecv[l, r].astype(F32)
        drecv[l, 0] = total.astype(BF)
        emit(drecv.at[l, 0], out)

    finish(1, gg2, gu2, gw2)
    finish_dense(1, gd2)
    grad_mixed = backward_combine(0, GR_ONE, grt1, gmb[0])
    dense_grad(0, xin[0], grad_mixed)
    dxb[...] = grad_input(grad_mixed, vm1)
    emit(dxb, dx_out)
    finish(0, gg1, gu1, gw1)
    finish_dense(0, gd1)

    for k in range(1, EP):
        for phase, buf in ((ROUTE, rt), (X_IN, xin), (DY, dyb), (Y_ONE, yb), (GM, gmb)):
            spread(phase, buf, k).wait_send()
        for phase, buf in ((O_ONE, oret), (GR_TWO, grt2), (GR_ONE, grt1)):
            giveback(phase, buf, k).wait_send()
    for l in range(2):
        for copy in pairs(l) + dense_copies(l):
            copy.wait_send()
    for copy in outs:
        copy.wait()


def solution(mesh):
    tok_spec = P(('dp', 'ep'), None)
    exp_spec = P('ep', None, None)
    layer_specs = (P(None, None), tok_spec, tok_spec, exp_spec, exp_spec, exp_spec)
    grad_specs = (P(('dp', 'ep'), None), P('ep', 'dp', None), P('ep', 'dp', None), P('ep', None, 'dp'))

    def local_step(tokens, dy_out, dense_w1, route_idx1, route_gate1, w_gate1, w_up1, w_down1, dense_w2, route_idx2, route_gate2, w_gate2, w_up2, w_down2):
        route = jnp.concatenate([route_idx1.astype(F32).T, route_idx2.astype(F32).T, route_gate1.T, route_gate2.T], axis=0)
        hbm = pl.BlockSpec(memory_space=pl.ANY)
        half = D // DP

        def sds(*shape):
            return jax.ShapeDtypeStruct(shape, BF)

        grads = (sds(32, D), sds(E_LOC, half, FF), sds(E_LOC, half, FF), sds(E_LOC, FF, half))
        vm = pltpu.VMEM
        dma = pltpu.SemaphoreType.DMA
        weights = [vm((D, D), BF), vm((E_LOC, D, FF), BF), vm((E_LOC, D, FF), BF), vm((E_LOC, FF, D), BF)]
        spread_buf = vm((EP, TOK, D), BF)
        ret_buf = vm((2 * EP - 1, TOK, D), BF)
        scratch = [vm((EP, 8, TOK), F32), spread_buf, spread_buf, spread_buf, spread_buf, ret_buf, ret_buf, ret_buf]
        scratch += weights + weights
        scratch += [vm((TOK, TOK), BF), vm((2, EP, 8, TOK), jnp.int32), vm((2, EP, 8, TOK), F32), vm((2, 8, TOK), jnp.int32)]
        scratch += [vm((E_LOC, EP * CAP, D), BF)] * 3
        scratch += [vm((E_LOC, EP * CAP, FF), F32)] * 2
        scratch += [vm((E_LOC, EP * CAP, FF), BF)] * 3
        scratch += [vm((TOK, D), BF), vm((TOK, D), F32), vm((TOK, D), F32)]
        scratch += [vm((2, DP, E_LOC, half, FF), BF)] * 2 + [vm((2, DP, E_LOC, FF, half), BF)]
        scratch += [vm((2, E_LOC, half, FF), BF)] * 2 + [vm((2, E_LOC, FF, half), BF)]
        scratch += [vm((2, EP * DP, 32, D), BF), vm((2, EP * DP, 32, D), BF), vm((TOK, D), BF)]
        scratch += [dma((11,)), dma((8, EP)), dma((8, EP)), dma((2, 3)), dma((2, 3)), dma((2, 8)), dma((2, 8)), dma((9,))]
        return pl.pallas_call(
            kernel,
            out_shape=(sds(TOK, D),) + grads + grads,
            in_specs=[hbm] * 11,
            out_specs=(hbm,) * 9,
            scratch_shapes=scratch,
            name='moe_backward',
            compiler_params=pltpu.CompilerParams(collective_id=0, has_side_effects=True, vmem_limit_bytes=67043328),
        )(tokens, dy_out, route, dense_w1, w_gate1, w_up1, w_down1, dense_w2, w_gate2, w_up2, w_down2)

    return jax.shard_map(local_step, mesh=mesh, in_specs=(tok_spec, tok_spec) + layer_specs + layer_specs,
                         out_specs=(tok_spec,) + grad_specs + grad_specs, check_vma=False)
```

profile of v0, /device:TPU:0, one launch (start us, length us, event | category | flops | bytes accessed | tf_op | source)
XLA Modules:
  0.0 113.0 jit_solution(10651994008506539176)
XLA Ops:
  0.6 0.0 copy-start.8
  0.7 0.0 copy-start.9
  0.7 0.7 convert_bitcast_fusion
  1.4 0.0 copy-done.8
  1.4 0.0 copy-done.9
  1.4 0.6 pad_maximum_fusion.route
  2.0 101.7 %moe_backward.1 = (bf16[512,256]{1,0:T(8,128)(2,1)}, bf16[32,256]{1,0:T(8,128)(2,1)}, bf16[2,128,896]{2,1,0:T(8,128)(2,1)}, bf16[2,128,896]{2,1,0:T(8,128)(2,1)}...) custom-call(bf16[512,256]{1,0:T(8,128)(2,1)} %tokens.1, ...), custom_call_target="tpu_custom_call" | custom-call | tf_op jit(solution)/shard_map/moe_backward/pallas_call | solution.py:385
  103.7 0.0 copy-start.5
  103.7 0.0 copy-start.7
  103.7 1.7 %copy.32 = bf16[512,256]{1,0:T(8,128)(2,1)} copy(bf16[512,256]{1,0:T(8,128)(2,1)} %get-tuple-element.20) | data formatting | bytes 524288
  105.5 0.0 copy-done.7
  105.5 0.6 copy.33
  106.1 0.0 copy-done.5
  106.1 0.8 copy.34
  106.8 0.4 copy-done.4
  107.3 0.8 copy.35
  108.0 0.4 copy-done.3
  108.4 0.8 copy.36
  109.2 0.6 copy.37
  109.8 0.8 copy.38
  110.6 0.4 copy-done.1
  111.0 0.8 copy.39
  111.8 0.4 copy-done
  112.2 0.8 copy.40
  (8 shorter events, 0.0 us)
Async XLA Ops:
  0.6 0.7 copy-start.8
  0.7 0.7 copy-start.9
  103.7 2.4 %copy-start.5 = (bf16[2,128,896]{2,1,0:T(8,128)(2,1)S(1)}, bf16[2,128,896]{2,1,0:T(8,128)(2,1)}, u32[]{:S(2)}) copy-start(bf16[2,128,896]{2,1,0:T(8,128)(2,1)} %get-tuple-element.22) | copy-start | bytes 1376260
  103.7 1.7 %copy-start.7 = (bf16[32,256]{1,0:T(8,128)(2,1)S(1)}, bf16[32,256]{1,0:T(8,128)(2,1)}, u32[]{:S(2)}) copy-start(bf16[32,256]{1,0:T(8,128)(2,1)} %get-tuple-element.21) | copy-start | bytes 49156
  106.1 1.2 %copy-start.4 = (bf16[2,128,896]{2,1,0:T(8,128)(2,1)S(1)}, bf16[2,128,896]{2,1,0:T(8,128)(2,1)}, u32[]{:S(2)}) copy-start(bf16[2,128,896]{2,1,0:T(8,128)(2,1)} %get-tuple-element.23) | copy-start | bytes 1376260
  107.3 1.2 %copy-start.3 = (bf16[2,896,128]{2,1,0:T(8,128)(2,1)S(1)}, bf16[2,896,128]{2,1,0:T(8,128)(2,1)}, u32[]{:S(2)}) copy-start(bf16[2,896,128]{2,1,0:T(8,128)(2,1)} %get-tuple-element.24) | copy-start | bytes 1376260
  108.4 0.8 copy-start.6
  108.4 1.4 %copy-start.2 = (bf16[2,128,896]{2,1,0:T(8,128)(2,1)S(1)}, bf16[2,128,896]{2,1,0:T(8,128)(2,1)}, u32[]{:S(2)}) copy-start(bf16[2,128,896]{2,1,0:T(8,128)(2,1)} %get-tuple-element.26) | copy-start | bytes 1376260
  109.8 1.2 %copy-start.1 = (bf16[2,128,896]{2,1,0:T(8,128)(2,1)S(1)}, bf16[2,128,896]{2,1,0:T(8,128)(2,1)}, u32[]{:S(2)}) copy-start(bf16[2,128,896]{2,1,0:T(8,128)(2,1)} %get-tuple-element.27) | copy-start | bytes 1376260
  111.0 1.2 %copy-start = (bf16[2,896,128]{2,1,0:T(8,128)(2,1)S(1)}, bf16[2,896,128]{2,1,0:T(8,128)(2,1)}, u32[]{:S(2)}) copy-start(bf16[2,896,128]{2,1,0:T(8,128)(2,1)} %get-tuple-element.28) | copy-start | bytes 1376260
where the time goes:
time: 113 us
  Pallas kernels  102 us (90%)
  local copies, waits for them, and re-layouts  9.23 us (8%)
  other arithmetic  1.34 us (1%)
    pallas_call x1, Pallas kernels, local_step(): pl.pallas_call(kernel, out_shape=(sds(TOK, D),) + grads + grads, in_specs...  102 us
    unnamed x29, local copies, waits for them, and re-layouts  9.23 us

commit v1 on v0

v1 whole, which is shorter than its diff:
```python
import jax
import jax.numpy as jnp
from jax import lax
from jax.experimental import pallas as pl
from jax.experimental.pallas import tpu as pltpu
from jax.sharding import PartitionSpec as P

MESH = pl.DeviceIdType.MESH
BF = jnp.bfloat16
F32 = jnp.float32
NN = ((1,), (0,))
NT = ((1,), (1,))
TN = ((0,), (0,))
EP = 4
DP = 2
E_LOC = 2
TOK = 512
CAP = 256
D = 256
FF = 896
X_IN, DY, Y_ONE, GM = range(4)
O_ONE, GR_TWO, GR_ONE = range(3)


def dot(a, b, dims=NN):
    return lax.dot_general(a, b, (dims, ((), ())), preferred_element_type=F32)


def place(k):
    return k + 3 * ((k + 3) // 4)


def onehot(key_row):
    rows = lax.broadcasted_iota(jnp.int32, (CAP, TOK), 0)
    return jnp.where(rows == key_row, 1.0, 0.0).astype(BF)


def gate_column(key_row, gate_row):
    rows = lax.broadcasted_iota(jnp.int32, (CAP, TOK), 0)
    return jnp.sum(jnp.where(rows == key_row, gate_row, 0.0), axis=1, keepdims=True)


def kernel(tokens, dy, idx1, idx2, gate1, gate2, m1, g1, u1, w1, m2, g2, u2, w2,
           dx_out, own_g, own_u, own_w, got_g, got_u, got_w, dense_out,
           ibuf, gbuf, rt, xin, dyb, yb, gmb, oret, grt2, grt1,
           vm1, vg1, vu1, vw1, vm2, vg2, vu2, vw2,
           tri, keys, gates, keyj, x1, x2, gout, a1, b1, hb, ga, gb, u_home, p0, p1,
           wg, wu, wd, dpart, dxb,
           loc_sem, rt_send, rt_recv, ag_send, ag_recv, ret_send, ret_recv, dp_send, dp_recv, all_send, all_recv, out_sem):
    me = lax.axis_index('ep')
    dp = lax.axis_index('dp')
    flat = dp * EP + me
    other = 1 - dp

    def partner(k):
        return (me // 2 + k // 2) % 2 * 2 + (me + k) % 2

    loads = [(idx1, ibuf.at[0]), (idx2, ibuf.at[1]), (gate1, gbuf.at[0]), (gate2, gbuf.at[1]), (tokens, xin.at[0]),
             (m1, vm1), (g1, vg1), (u1, vu1), (w1, vw1), (dy, dyb.at[0]), (m2, vm2), (g2, vg2), (u2, vu2), (w2, vw2)]
    loads = [pltpu.make_async_copy(src, dst, loc_sem.at[n]) for n, (src, dst) in enumerate(loads)]
    for copy in loads:
        copy.start()

    barrier = pltpu.get_barrier_semaphore()
    for r in range(1, EP * DP):
        peer = (flat + r) % (EP * DP)
        pl.semaphore_signal(barrier, inc=1, device_id={'ep': peer % EP, 'dp': peer // EP}, device_id_type=MESH)

    for copy in loads[:4]:
        copy.wait()
    rt[0] = jnp.concatenate([ibuf[0].astype(F32), ibuf[1].astype(F32), gbuf[0], gbuf[1]], axis=0)
    loads[4].wait()
    pl.semaphore_wait(barrier, EP * DP - 1)

    def remote(src, dst, send, recv, k):
        return pltpu.make_async_remote_copy(src_ref=src, dst_ref=dst, send_sem=send, recv_sem=recv,
                                            device_id={'ep': partner(k)}, device_id_type=MESH)

    def tell(k):
        return remote(rt.at[0], rt.at[k], rt_send.at[k], rt_recv.at[k], k)

    def half(h):
        return pl.ds(h * CAP, CAP)

    def ship(phase, buf, k, piece):
        rows = half(piece if k == 1 else 1 - piece)
        return remote(buf.at[0, rows], buf.at[k, rows], ag_send.at[phase, k, piece], ag_recv.at[phase, k, piece], k)

    def relay(phase, buf, via):
        rows = half(via - 1)
        return remote(buf.at[via, rows], buf.at[3, rows], ag_send.at[phase, 3, via - 1], ag_recv.at[phase, 3, via - 1], 3 - via)

    def spread(phase, buf):
        for piece in range(2):
            for k in (1, 2):
                ship(phase, buf, k, piece).start()

    def pass_on(phase, buf):
        for via in (1, 2):
            ship(phase, buf, via, 0).wait_recv()
            relay(phase, buf, via).start()

    def arrive(phase, buf, k):
        for near in (1, 2):
            @pl.when(k == near)
            def _():
                ship(phase, buf, near, 1).wait_recv()

        @pl.when(k == 3)
        def _():
            for via in (1, 2):
                relay(phase, buf, via).wait_recv()

    def giveback(phase, buf, k, el):
        rows = pl.ds(pl.multiple_of(el * CAP, CAP), CAP)
        return remote(buf.at[k, rows], buf.at[k + 3, rows], ret_send.at[phase, k, el], ret_recv.at[phase, k, el], k)

    for k in range(1, EP):
        tell(k).start()
    spread(X_IN, xin)

    tri[...] = jnp.where(lax.broadcasted_iota(jnp.int32, (TOK, TOK), 0) < lax.broadcasted_iota(jnp.int32, (TOK, TOK), 1), 1.0, 0.0).astype(BF)
    expert = lax.broadcasted_iota(jnp.int32, (E_LOC * EP, TOK), 0).astype(F32)

    def make_keys(k):
        info = rt[k]
        for l in range(2):
            hit0 = info[2 * l:2 * l + 1] == expert
            hit1 = info[2 * l + 1:2 * l + 2] == expert
            both = jnp.where(hit0, 1.0, jnp.where(hit1, 1.0, 0.0))
            rank = dot(both.astype(BF), tri[...]).astype(jnp.int32)
            keys[l, k] = jnp.where(both > 0.5, rank, -1)
            gates[l, k] = jnp.where(hit0, info[4 + 2 * l:5 + 2 * l], jnp.where(hit1, info[5 + 2 * l:6 + 2 * l], 0.0))
        return info

    info = make_keys(0)
    for j in range(2):
        keyj[j] = jnp.where(info[j:j + 1] == expert, keys[0, 0], -1)
    for copy in loads[5:9]:
        copy.wait()

    def mixed(x, m):
        return (x.astype(F32) + dot(x, m[...])).astype(BF)

    def forward_one(k, carry):
        @pl.when(k == 1)
        def _():
            pass_on(X_IN, xin)

        @pl.when(k > 0)
        def _():
            tell(k).wait_recv()
            make_keys(k)

        arrive(X_IN, xin, k)
        u = mixed(xin[k], vm1)

        @pl.when(k == 0)
        def _():
            u_home[...] = u

        def one(el, c):
            rows = pl.ds(pl.multiple_of(k * CAP, CAP), CAP)
            key = keys[0, k, pl.ds(me * E_LOC + el, 1), :]
            x = dot(onehot(key), u).astype(BF)
            x1[el, rows] = x
            a = dot(x, vg1[el])
            b = dot(x, vu1[el])
            a1[el, rows] = a
            b1[el, rows] = b
            h = (a * (0.5 * jnp.tanh(0.5 * a) + 0.5) * b).astype(BF)
            oret[k, pl.ds(pl.multiple_of(el * CAP, CAP), CAP)] = dot(h, vw1[el]).astype(BF)

            @pl.when(k > 0)
            def _():
                giveback(O_ONE, oret, k, el).start()
            return c

        lax.fori_loop(0, E_LOC, one, 0)
        return carry

    lax.fori_loop(0, EP, forward_one, 0)
    for copy in loads[9:]:
        copy.wait()
    spread(DY, dyb)

    p0[...] = jnp.zeros_like(p0)
    p1[...] = jnp.zeros_like(p1)

    def combine_one(k, carry):
        def one(el, c):
            @pl.when(k > 0)
            def _():
                giveback(O_ONE, oret, k, el).wait_recv()

            rows = oret[place(k), pl.ds(pl.multiple_of(el * CAP, CAP), CAP)]
            e = partner(k) * E_LOC + el
            p0[...] += dot(onehot(keyj[0, pl.ds(e, 1), :]), rows, TN)
            p1[...] += dot(onehot(keyj[1, pl.ds(e, 1), :]), rows, TN)
            return c

        lax.fori_loop(0, E_LOC, one, 0)
        return carry

    lax.fori_loop(0, EP, combine_one, 0)
    gcol0 = jnp.transpose(jnp.broadcast_to(rt[0, 4:5], (8, TOK)))[:, :1]
    gcol1 = jnp.transpose(jnp.broadcast_to(rt[0, 5:6], (8, TOK)))[:, :1]
    yb[0] = (u_home[...].astype(F32) + (gcol0 * p0[...] + gcol1 * p1[...])).astype(BF)
    spread(Y_ONE, yb)

    def expert_backward(k, el, a, b, vg, vu, vw, phase, ret):
        rows = pl.ds(pl.multiple_of(k * CAP, CAP), CAP)
        dh = dot(gout[el, rows], vw[el], NT).astype(BF).astype(F32)
        sig = 0.5 * jnp.tanh(0.5 * a) + 0.5
        s = a * sig
        hb[el, rows] = (s * b).astype(BF)
        grad_a = (dh * b * (sig + s * (1.0 - sig))).astype(BF)
        grad_b = (dh * s).astype(BF)
        ga[el, rows] = grad_a
        gb[el, rows] = grad_b
        back = dot(grad_a, vg[el], NT) + dot(grad_b, vu[el], NT)
        ret[k, pl.ds(pl.multiple_of(el * CAP, CAP), CAP)] = back.astype(BF)

        @pl.when(k > 0)
        def _():
            giveback(phase, ret, k, el).start()

    def layer_two(k, carry):
        @pl.when(k == 1)
        def _():
            pass_on(DY, dyb)
            pass_on(Y_ONE, yb)

        arrive(DY, dyb, k)
        arrive(Y_ONE, yb, k)
        u = mixed(yb[k], vm2)

        def one(el, c):
            rows = pl.ds(pl.multiple_of(k * CAP, CAP), CAP)
            e = pl.ds(me * E_LOC + el, 1)
            key = keys[1, k, e, :]
            pick = onehot(key)
            x = dot(pick, u).astype(BF)
            x2[el, rows] = x
            gout[el, rows] = (dot(pick, dyb[k]) * gate_column(key, gates[1, k, e, :])).astype(BF)
            a = dot(x, vg2[el])
            b = dot(x, vu2[el])
            expert_backward(k, el, a, b, vg2, vu2, vw2, GR_TWO, grt2)
            return c

        lax.fori_loop(0, E_LOC, one, 0)
        return carry

    lax.fori_loop(0, EP, layer_two, 0)

    stacks = ((wg, own_g, got_g), (wu, own_u, got_u), (wd, own_w, got_w))

    def pairs(l):
        return [pltpu.make_async_remote_copy(src_ref=part.at[l, other], dst_ref=got.at[l], send_sem=dp_send.at[l, n],
                                             recv_sem=dp_recv.at[l, n], device_id={'dp': other}, device_id_type=MESH)
                for n, (part, own, got) in enumerate(stacks)]

    outs = []

    def emit(src, dst):
        copy = pltpu.make_async_copy(src, dst, out_sem.at[len(outs)])
        copy.start()
        outs.append(copy)

    def weight_grads(l, x_all):
        half_d = D // DP

        def one(el, c):
            x = x_all[el]
            go = gout[el]
            down = dot(hb[el], go, TN).astype(BF)
            gate = dot(x, ga[el], TN).astype(BF)
            up = dot(x, gb[el], TN).astype(BF)
            for d in range(DP):
                wd[l, d, el] = down[:, d * half_d:(d + 1) * half_d]
                wg[l, d, el] = gate[d * half_d:(d + 1) * half_d]
                wu[l, d, el] = up[d * half_d:(d + 1) * half_d]
            return c

        lax.fori_loop(0, E_LOC, one, 0)
        for copy in pairs(l):
            copy.start()
        for part, own, got in stacks:
            emit(part.at[l, dp], own.at[l])

    weight_grads(1, x2)

    def backward_combine(l, phase, ret, grad_y):
        p0[...] = jnp.zeros_like(p0)

        def step(k, carry):
            def one(el, c):
                @pl.when(k > 0)
                def _():
                    giveback(phase, ret, k, el).wait_recv()

                rows = ret[place(k), pl.ds(pl.multiple_of(el * CAP, CAP), CAP)]
                e = partner(k) * E_LOC + el
                p0[...] += dot(onehot(keys[l, 0, pl.ds(e, 1), :]), rows, TN)
                return c

            lax.fori_loop(0, E_LOC, one, 0)
            return carry

        lax.fori_loop(0, EP, step, 0)
        return (grad_y.astype(F32) + p0[...]).astype(BF)

    def grad_input(grad_mixed, m):
        return (grad_mixed.astype(F32) + dot(grad_mixed, m[...], NT)).astype(BF)

    def dense_copies(l):
        copies = []
        for r in range(1, EP * DP):
            peer = (flat + r) % (EP * DP)
            copies.append(pltpu.make_async_remote_copy(
                src_ref=dpart.at[l, peer], dst_ref=dense_out.at[l, r], send_sem=all_send.at[l, r], recv_sem=all_recv.at[l, r],
                device_id={'ep': peer % EP, 'dp': peer // EP}, device_id_type=MESH))
        return copies

    def dense_grad(l, x, grad_mixed):
        part = dot(x, grad_mixed, TN).astype(BF)
        for q in range(EP * DP):
            dpart[l, q] = part[q * 32:(q + 1) * 32]
        for copy in dense_copies(l):
            copy.start()
        emit(dpart.at[l, flat], dense_out.at[l, 0])

    grad_mixed = backward_combine(1, GR_TWO, grt2, dyb[0])
    gmb[0] = grad_input(grad_mixed, vm2)
    spread(GM, gmb)
    dense_grad(1, yb[0], grad_mixed)

    def backward_one(k, carry):
        @pl.when(k == 1)
        def _():
            pass_on(GM, gmb)

        arrive(GM, gmb, k)

        def one(el, c):
            rows = pl.ds(pl.multiple_of(k * CAP, CAP), CAP)
            e = pl.ds(me * E_LOC + el, 1)
            key = keys[0, k, e, :]
            gout[el, rows] = (dot(onehot(key), gmb[k]) * gate_column(key, gates[0, k, e, :])).astype(BF)
            expert_backward(k, el, a1[el, rows], b1[el, rows], vg1, vu1, vw1, GR_ONE, grt1)
            return c

        lax.fori_loop(0, E_LOC, one, 0)
        return carry

    lax.fori_loop(0, EP, backward_one, 0)
    weight_grads(0, x1)
    grad_mixed = backward_combine(0, GR_ONE, grt1, gmb[0])
    dense_grad(0, xin[0], grad_mixed)
    dxb[...] = grad_input(grad_mixed, vm1)
    emit(dxb, dx_out)

    for k in range(1, EP):
        tell(k).wait_send()
        for phase, buf in ((O_ONE, oret), (GR_TWO, grt2), (GR_ONE, grt1)):
            for el in range(E_LOC):
                giveback(phase, buf, k, el).wait_send()
    for phase, buf in ((X_IN, xin), (DY, dyb), (Y_ONE, yb), (GM, gmb)):
        for k in (1, 2):
            for piece in range(2):
                ship(phase, buf, k, piece).wait_send()
            relay(phase, buf, k).wait_send()
    for l in range(2):
        for copy in pairs(l) + dense_copies(l):
            copy.wait()
    for copy in outs:
        copy.wait()


def finish(dx, own_g, own_u, own_w, got_g, got_u, got_w, dense,
           dx_out, gd1, gg1, gu1, gw1, gd2, gg2, gu2, gw2,
           vx, vog, vou, vow, vrg, vru, vrw, vd, vsum, in_sem, out_sem):
    loads = []

    def load(src, dst):
        copy = pltpu.make_async_copy(src, dst, in_sem.at[len(loads)])
        copy.start()
        loads.append(copy)
        return copy

    dense_in = load(dense, vd)
    dx_in = load(dx, vx)
    stacks = []
    for l, outs in enumerate(((gg1, gu1, gw1), (gg2, gu2, gw2))):
        for own, got, vo, vr, out in zip((own_g, own_u, own_w), (got_g, got_u, got_w), (vog, vou, vow), (vrg, vru, vrw), outs):
            stacks.append((load(own.at[l], vo.at[l]), load(got.at[l], vr.at[l]), vo.at[l], vr.at[l], out))
    stores = []

    def store(src, dst):
        copy = pltpu.make_async_copy(src, dst, out_sem.at[len(stores)])
        copy.start()
        stores.append(copy)

    dense_in.wait()
    for l, out in enumerate((gd1, gd2)):
        vsum[l] = jnp.sum(vd[l].astype(F32), axis=0).astype(BF)
        store(vsum.at[l], out)
    dx_in.wait()
    store(vx, dx_out)
    for first, second, vo, vr, out in stacks:
        first.wait()
        second.wait()
        vo[...] = (vo[...].astype(F32) + vr[...].astype(F32)).astype(BF)
        store(vo, out)
    for copy in stores:
        copy.wait()


def solution(mesh):
    tok_spec = P(('dp', 'ep'), None)
    exp_spec = P('ep', None, None)
    layer_specs = (P(None, None), tok_spec, tok_spec, exp_spec, exp_spec, exp_spec)
    grad_specs = (P(('dp', 'ep'), None), P('ep', 'dp', None), P('ep', 'dp', None), P('ep', None, 'dp'))

    def local_step(tokens, dy_out, dense_w1, route_idx1, route_gate1, w_gate1, w_up1, w_down1, dense_w2, route_idx2, route_gate2, w_gate2, w_up2, w_down2):
        hbm = pl.BlockSpec(memory_space=pl.ANY)
        half = D // DP

        def sds(*shape):
            return jax.ShapeDtypeStruct(shape, BF)

        grads = (sds(32, D), sds(E_LOC, half, FF), sds(E_LOC, half, FF), sds(E_LOC, FF, half))
        stacks = (sds(2, E_LOC, half, FF), sds(2, E_LOC, half, FF), sds(2, E_LOC, FF, half))
        vm = pltpu.VMEM
        dma = pltpu.SemaphoreType.DMA
        weights = [vm((D, D), BF), vm((E_LOC, D, FF), BF), vm((E_LOC, D, FF), BF), vm((E_LOC, FF, D), BF)]
        spread_buf = vm((EP, TOK, D), BF)
        ret_buf = vm((2 * EP - 1, TOK, D), BF)
        scratch = [vm((2, 2, TOK), jnp.int32), vm((2, 2, TOK), F32)]
        scratch += [vm((EP, 8, TOK), F32), spread_buf, spread_buf, spread_buf, spread_buf, ret_buf, ret_buf, ret_buf]
        scratch += weights + weights
        scratch += [vm((TOK, TOK), BF), vm((2, EP, 8, TOK), jnp.int32), vm((2, EP, 8, TOK), F32), vm((2, 8, TOK), jnp.int32)]
        scratch += [vm((E_LOC, EP * CAP, D), BF)] * 3
        scratch += [vm((E_LOC, EP * CAP, FF), F32)] * 2
        scratch += [vm((E_LOC, EP * CAP, FF), BF)] * 3
        scratch += [vm((TOK, D), BF), vm((TOK, D), F32), vm((TOK, D), F32)]
        scratch += [vm((2, DP, E_LOC, half, FF), BF)] * 2 + [vm((2, DP, E_LOC, FF, half), BF)]
        scratch += [vm((2, EP * DP, 32, D), BF), vm((TOK, D), BF)]
        scratch += [dma((14,)), dma((EP,)), dma((EP,)), dma((4, EP, 2)), dma((4, EP, 2)), dma((3, EP, 2)), dma((3, EP, 2)),
                    dma((2, 3)), dma((2, 3)), dma((2, 8)), dma((2, 8)), dma((9,))]
        parts = pl.pallas_call(
            kernel,
            out_shape=(sds(TOK, D),) + stacks + stacks + (sds(2, EP * DP, 32, D),),
            in_specs=[hbm] * 14,
            out_specs=(hbm,) * 8,
            scratch_shapes=scratch,
            name='moe_backward',
            compiler_params=pltpu.CompilerParams(collective_id=0, has_side_effects=True, vmem_limit_bytes=67043328),
        )(tokens, dy_out, route_idx1.T, route_idx2.T, route_gate1.T, route_gate2.T,
          dense_w1, w_gate1, w_up1, w_down1, dense_w2, w_gate2, w_up2, w_down2)
        return pl.pallas_call(
            finish,
            out_shape=(sds(TOK, D),) + grads + grads,
            in_specs=[hbm] * 8,
            out_specs=(hbm,) * 9,
            scratch_shapes=[vm(p.shape, BF) for p in parts] + [vm((2, 32, D), BF), dma((14,)), dma((9,))],
            name='finish',
        )(*parts)

    return jax.shard_map(local_step, mesh=mesh, in_specs=(tok_spec, tok_spec) + layer_specs + layer_specs,
                         out_specs=(tok_spec,) + grad_specs + grad_specs, check_vma=False)
```

time: 113 us -> 91.2 us (0.81)
  Pallas kernels: 102 us -> 90.4 us
  local copies, waits for them, and re-layouts: 9.23 us -> 0 us
  other arithmetic: 1.34 us -> 0 us
    pallas_call x1 -> x2, Pallas kernels: 102 us -> 90.4 us  [the longest x1 85.9 us: local_step(): pl.pallas_call(kernel, out_shape=(sds(TOK, D),) + stacks + stacks + (sds(...]
    unnamed x29 -> x0, local copies, waits for them, and re-layouts: 9.23 us -> none
where the time goes in v1:
time: 91.2 us; the launch traced here: 91 us
  Pallas kernels  90.4 us (99%)
    pallas_call x1, Pallas kernels, local_step(): pl.pallas_call(kernel, out_shape=(sds(TOK, D),) + stacks + stacks + (sds(...  85.9 us
    pallas_call x1, Pallas kernels, local_step(): pl.pallas_call(finish, out_shape=(sds(TOK, D),) + grads + grads, in_specs...  4.45 us

profile of v1, /device:TPU:0, one launch (start us, length us, event | category | flops | bytes accessed | tf_op | source)
XLA Modules:
  0.0 91.0 jit_solution(1588115543795747225)
XLA Ops:
  0.6 85.9 %moe_backward.1 = (bf16[512,256]{1,0:T(8,128)(2,1)}, bf16[2,2,128,896]{3,2,1,0:T(8,128)(2,1)}, bf16[2,2,128,896]{3,2,1,0:T(8,128)(2,1)}, bf16[2,2,896,128]{3,2,1...) custom-call(bf16[512,256]{1,0:T(8,128)(2,1)} %tokens.1, ...), custom_call_target="tpu_custom_call" | custom-call | tf_op jit(solution)/shard_map/moe_backward/pallas_call | solution.py:451
  86.6 4.5 %finish.1 = (bf16[512,256]{1,0:T(8,128)(2,1)}, bf16[32,256]{1,0:T(8,128)(2,1)}, bf16[2,128,896]{2,1,0:T(8,128)(2,1)}, bf16[2,128,896]{2,1,0:T(8,128)(2,1)}, bf16...) custom-call(bf16[512,256]{1,0:T(8,128)(2,1)} %get-tuple-element.17.d, ...), custom_call_target="tpu_custom_call" | custom-call | tf_op jit(solution)/shard_map/finish/pallas_call | solution.py:461

commit v2 on v1

v2 whole, which is shorter than its diff:
```python
import jax
import jax.numpy as jnp
from jax import lax
from jax.experimental import pallas as pl
from jax.experimental.pallas import tpu as pltpu
from jax.sharding import PartitionSpec as P

MESH = pl.DeviceIdType.MESH
BF = jnp.bfloat16
F32 = jnp.float32
NN = ((1,), (0,))
NT = ((1,), (1,))
TN = ((0,), (0,))
EP = 4
DP = 2
E_LOC = 2
TOK = 512
CAP = 256
D = 256
FF = 896
LANES = 128
TILES = FF // LANES
VMEM_LIMIT = 54 * 1024 * 1024
X_IN, DY, Y_ONE, GM = range(4)
O_ONE, GR_TWO, GR_ONE = range(3)


def dot(a, b, dims=NN):
    return lax.dot_general(a, b, (dims, ((), ())), preferred_element_type=F32)


def place(k):
    return k + 3 * ((k + 3) // 4)


def unit(i):
    q = i // 2
    mid = (q + 1) // 2 % 2
    return mid * (1 + i % 2) + (1 - mid) * q, mid * (q - 1) + (1 - mid) * (i % 2)


def onehot(key_row):
    rows = lax.broadcasted_iota(jnp.int32, (CAP, TOK), 0)
    return jnp.where(rows == key_row, 1.0, 0.0).astype(BF)


def gate_column(key_row, gate_row):
    rows = lax.broadcasted_iota(jnp.int32, (CAP, TOK), 0)
    return jnp.sum(jnp.where(rows == key_row, gate_row, 0.0), axis=1, keepdims=True)


def kernel(tokens, dy, idx1, idx2, gate1, gate2, m1, g1, u1, w1, m2, g2, u2, w2,
           dx_out, wg, wu, wd, got_g, got_u, got_w, dpart, dense_got,
           ibuf, gbuf, rt, xin, dyb, yb, gmb, oret, grt2, grt1,
           vm1, vgu1, vw1, vm2, vgu2, vw2,
           tri, keys, gates, keyj, picks, x1, x2, gout, ab1, hb, gab, ub, p0, p1,
           loc_sem, rt_send, rt_recv, ag_send, ag_recv, ret_send, ret_recv, dp_send, dp_recv, all_send, all_recv):
    me = lax.axis_index('ep')
    dp = lax.axis_index('dp')
    flat = dp * EP + me
    other = 1 - dp

    barrier = pltpu.get_barrier_semaphore()
    for r in range(1, EP * DP):
        peer = (flat + r) % (EP * DP)
        pl.semaphore_signal(barrier, inc=1, device_id={'ep': peer % EP, 'dp': peer // EP}, device_id_type=MESH)

    def partner(k):
        return (me // 2 + k // 2) % 2 * 2 + (me + k) % 2

    def weight_loads(m, g, u, w, vm, vgu, vw):
        pieces = [(m, vm), (w, vw)]
        for n in range(TILES):
            cols = pl.ds(n * LANES, LANES)
            pieces += [(g.at[:, :, cols], vgu.at[:, n, :, pl.ds(0, LANES)]), (u.at[:, :, cols], vgu.at[:, n, :, pl.ds(LANES, LANES)])]
        return pieces

    loads = [(idx1, ibuf.at[0]), (idx2, ibuf.at[1]), (gate1, gbuf.at[0]), (gate2, gbuf.at[1]), (tokens, xin.at[0]), (dy, dyb.at[0])]
    loads += weight_loads(m1, g1, u1, w1, vm1, vgu1, vw1)
    loads_one = len(loads)
    loads += weight_loads(m2, g2, u2, w2, vm2, vgu2, vw2)
    loads = [pltpu.make_async_copy(src, dst, loc_sem.at[n]) for n, (src, dst) in enumerate(loads)]
    for copy in loads:
        copy.start()

    for copy in loads[:4]:
        copy.wait()
    rt[0] = jnp.concatenate([ibuf[0].astype(F32), ibuf[1].astype(F32), gbuf[0], gbuf[1]], axis=0)
    loads[4].wait()
    pl.semaphore_wait(barrier, EP * DP - 1)

    def remote(src, dst, send, recv, k):
        return pltpu.make_async_remote_copy(src_ref=src, dst_ref=dst, send_sem=send, recv_sem=recv,
                                            device_id={'ep': partner(k)}, device_id_type=MESH)

    def tell(k):
        return remote(rt.at[0], rt.at[k], rt_send.at[k], rt_recv.at[k], k)

    def half(h):
        return pl.ds(h * CAP, CAP)

    def ship(phase, buf, k, piece):
        rows = half(piece if k == 1 else 1 - piece)
        return remote(buf.at[0, rows], buf.at[k, rows], ag_send.at[phase, k, piece], ag_recv.at[phase, k, piece], k)

    def relay(phase, buf, via):
        rows = half(via - 1)
        return remote(buf.at[via, rows], buf.at[3, rows], ag_send.at[phase, 3, via - 1], ag_recv.at[phase, 3, via - 1], 3 - via)

    def spread(phase, buf):
        for piece in range(2):
            for k in (1, 2):
                ship(phase, buf, k, piece).start()

    def pass_on(phase, buf):
        for via in (1, 2):
            ship(phase, buf, via, 0).wait_recv()
            relay(phase, buf, via).start()

    def arrive(phase, buf, k):
        for near in (1, 2):
            @pl.when(k == near)
            def _():
                ship(phase, buf, near, 1).wait_recv()

        @pl.when(k == 3)
        def _():
            for via in (1, 2):
                relay(phase, buf, via).wait_recv()

    def giveback(phase, buf, k, el):
        rows = pl.ds(pl.multiple_of(el * CAP, CAP), CAP)
        return remote(buf.at[k, rows], buf.at[k + 3, rows], ret_send.at[phase, k, el], ret_recv.at[phase, k, el], k)

    for k in range(1, EP):
        tell(k).start()

    @pl.when(dp == 1)
    def _():
        loads[5].wait()
        spread(DY, dyb)

    spread(X_IN, xin)

    tri[...] = jnp.where(lax.broadcasted_iota(jnp.int32, (TOK, TOK), 0) < lax.broadcasted_iota(jnp.int32, (TOK, TOK), 1), 1.0, 0.0).astype(BF)
    expert = lax.broadcasted_iota(jnp.int32, (E_LOC * EP, TOK), 0).astype(F32)

    def make_keys(k):
        info = rt[k]
        for l in range(2):
            hit0 = info[2 * l:2 * l + 1] == expert
            hit1 = info[2 * l + 1:2 * l + 2] == expert
            both = jnp.where(hit0, 1.0, jnp.where(hit1, 1.0, 0.0))
            rank = dot(both.astype(BF), tri[...]).astype(jnp.int32)
            keys[l, k] = jnp.where(both > 0.5, rank, -1)
            gates[l, k] = jnp.where(hit0, info[4 + 2 * l:5 + 2 * l], jnp.where(hit1, info[5 + 2 * l:6 + 2 * l], 0.0))
        return info

    info = make_keys(0)
    for j in range(2):
        keyj[j] = jnp.where(info[j:j + 1] == expert, keys[0, 0], -1)
    for copy in loads[6:loads_one]:
        copy.wait()

    def build_picks(*sources):
        slots = lax.broadcasted_iota(jnp.int32, (TOK, CAP), 1)
        for j, source in enumerate(sources):
            rows = [source[pl.ds(partner(k) * E_LOC + el, 1), :] for k in range(EP) for el in range(E_LOC)]
            cols = jnp.transpose(jnp.concatenate(rows, axis=0))
            for r in range(EP * E_LOC):
                picks[j, :, r * CAP:(r + 1) * CAP] = jnp.where(slots == cols[:, r:r + 1], 1.0, 0.0).astype(BF)

    def picked(j, ret, last):
        if last:
            return dot(picks[j, :, 3 * TOK:], ret[6])
        return dot(picks[j, :, :TOK], ret[0]) + dot(picks[j, :, TOK:3 * TOK], ret[4:6].reshape(2 * TOK, D))

    def silu_parts(a):
        sig = 0.5 * jnp.tanh(0.5 * a) + 0.5
        return sig, a * sig

    def groups():
        return [range(n, min(n + 2, TILES)) for n in range(0, TILES, 2)]

    def mixed(x, m):
        return (x.astype(F32) + dot(x, m[...])).astype(BF)

    def forward_one(i, carry):
        k, el = unit(i)

        @pl.when(i == 2)
        def _():
            build_picks(keyj.at[0], keyj.at[1])

            @pl.when(dp == 1)
            def _():
                pass_on(DY, dyb)

            pass_on(X_IN, xin)

        @pl.when(el == 0)
        def _():
            @pl.when(k > 0)
            def _():
                tell(k).wait_recv()
                make_keys(k)

            arrive(X_IN, xin, k)
            ub[k] = mixed(xin[k], vm1)

        rows = pl.ds(pl.multiple_of(k * CAP, CAP), CAP)
        key = keys[0, k, pl.ds(me * E_LOC + el, 1), :]
        x = dot(onehot(key), ub[k]).astype(BF)
        x1[el, rows] = x
        out = jnp.zeros((CAP, D), F32)
        for group in groups():
            h = []
            for n in group:
                ab = dot(x, vgu1[el, n])
                ab1[el, n, rows] = ab
                h.append((silu_parts(ab[:, :LANES])[1] * ab[:, LANES:]).astype(BF))
            out += dot(jnp.concatenate(h, axis=1), vw1[el, group[0] * LANES:(group[-1] + 1) * LANES])
        oret[k, pl.ds(pl.multiple_of(el * CAP, CAP), CAP)] = out.astype(BF)

        @pl.when(k > 0)
        def _():
            giveback(O_ONE, oret, k, el).start()
        return carry

    lax.fori_loop(0, EP * E_LOC, forward_one, 0)

    @pl.when(dp == 0)
    def _():
        loads[5].wait()
        spread(DY, dyb)

    for copy in loads[loads_one:]:
        copy.wait()

    def collect(phase, ret, ks):
        for k in ks:
            for el in range(E_LOC):
                giveback(phase, ret, k, el).wait_recv()

    collect(O_ONE, oret, (1, 2))
    p0[...] = picked(0, oret, False)
    p1[...] = picked(1, oret, False)
    gcol0 = jnp.transpose(jnp.broadcast_to(rt[0, 4:5], (8, TOK)))[:, :1]
    gcol1 = jnp.transpose(jnp.broadcast_to(rt[0, 5:6], (8, TOK)))[:, :1]
    collect(O_ONE, oret, (3,))
    out0 = p0[...] + picked(0, oret, True)
    out1 = p1[...] + picked(1, oret, True)
    yb[0] = (ub[0].astype(F32) + (gcol0 * out0 + gcol1 * out1)).astype(BF)
    spread(Y_ONE, yb)

    def expert_backward(k, el, first, vgu, vw, phase, ret):
        rows = pl.ds(pl.multiple_of(k * CAP, CAP), CAP)
        go = gout[el, rows]
        back = jnp.zeros((CAP, D), F32)
        for group in groups():
            cols = slice(group[0] * LANES, (group[-1] + 1) * LANES)
            grad_h = dot(go, vw[el, cols], NT).astype(BF).astype(F32)
            for n in group:
                ab = first(n)
                a, b = ab[:, :LANES], ab[:, LANES:]
                dh = grad_h[:, (n - group[0]) * LANES:(n - group[0] + 1) * LANES]
                sig, s = silu_parts(a)
                hb[el, rows, n * LANES:(n + 1) * LANES] = (s * b).astype(BF)
                grad_a = (dh * b * (sig + s * (1.0 - sig))).astype(BF)
                grad_b = (dh * s).astype(BF)
                grads = jnp.concatenate([grad_a, grad_b], axis=1)
                gab[el, n, rows] = grads
                back += dot(grads, vgu[el, n], NT)
        ret[k, pl.ds(pl.multiple_of(el * CAP, CAP), CAP)] = back.astype(BF)

        @pl.when(k > 0)
        def _():
            giveback(phase, ret, k, el).start()

    def layer_two(i, carry):
        k, el = unit(i)

        @pl.when(i == 2)
        def _():
            build_picks(keys.at[1, 0])

            @pl.when(dp == 0)
            def _():
                pass_on(DY, dyb)

            pass_on(Y_ONE, yb)

        @pl.when(el == 0)
        def _():
            arrive(DY, dyb, k)
            arrive(Y_ONE, yb, k)
            ub[k] = mixed(yb[k], vm2)

        rows = pl.ds(pl.multiple_of(k * CAP, CAP), CAP)
        e = pl.ds(me * E_LOC + el, 1)
        key = keys[1, k, e, :]
        pick = onehot(key)
        x = dot(pick, ub[k]).astype(BF)
        x2[el, rows] = x
        gout[el, rows] = (dot(pick, dyb[k]) * gate_column(key, gates[1, k, e, :])).astype(BF)
        expert_backward(k, el, lambda n: dot(x, vgu2[el, n]), vgu2, vw2, GR_TWO, grt2)
        return carry

    lax.fori_loop(0, EP * E_LOC, layer_two, 0)

    stacks = ((wg, got_g), (wu, got_u), (wd, got_w))

    def pairs(l):
        return [pltpu.make_async_remote_copy(src_ref=part.at[l, other], dst_ref=got.at[l], send_sem=dp_send.at[l, n],
                                             recv_sem=dp_recv.at[l, n], device_id={'dp': other}, device_id_type=MESH)
                for n, (part, got) in enumerate(stacks)]

    def weight_grads(l, x_all, el):
        half_d = D // DP
        x = x_all[el]
        down = dot(hb[el], gout[el], TN).astype(BF)
        for d in range(DP):
            wd[l, d, el] = down[:, d * half_d:(d + 1) * half_d]

        for n in range(TILES):
            cols = slice(n * LANES, (n + 1) * LANES)
            both = dot(x, gab[el, n], TN).astype(BF)
            for d in range(DP):
                rows = slice(d * half_d, (d + 1) * half_d)
                wg[l, d, el, :, cols] = both[rows, :LANES]
                wu[l, d, el, :, cols] = both[rows, LANES:]

    def send_weight_grads(l):
        for copy in pairs(l):
            copy.start()

    weight_grads(1, x2, 0)

    def backward_combine(phase, ret, grad_y):
        collect(phase, ret, (1, 2))
        p0[...] = picked(0, ret, False)
        collect(phase, ret, (3,))
        return (grad_y.astype(F32) + (p0[...] + picked(0, ret, True))).astype(BF)

    def grad_input(grad_mixed, m):
        return (grad_mixed.astype(F32) + dot(grad_mixed, m[...], NT)).astype(BF)

    def dense_copies(l):
        copies = []
        for r in range(1, EP * DP):
            peer = (flat + r) % (EP * DP)
            copies.append(pltpu.make_async_remote_copy(
                src_ref=dpart.at[l, peer], dst_ref=dense_got.at[l, r], send_sem=all_send.at[l, r], recv_sem=all_recv.at[l, r],
                device_id={'ep': peer % EP, 'dp': peer // EP}, device_id_type=MESH))
        return copies

    def dense_grad(l, x, grad_mixed):
        part = dot(x, grad_mixed, TN).astype(BF)
        for q in range(EP * DP):
            dpart[l, q] = part[q * 32:(q + 1) * 32]
        for copy in dense_copies(l):
            copy.start()

    grad_mixed = backward_combine(GR_TWO, grt2, dyb[0])
    gmb[0] = grad_input(grad_mixed, vm2)
    spread(GM, gmb)
    weight_grads(1, x2, 1)
    send_weight_grads(1)
    dense_grad(1, yb[0], grad_mixed)

    def backward_one(i, carry):
        k, el = unit(i)

        @pl.when(i == 2)
        def _():
            build_picks(keys.at[0, 0])

        @pl.when(i == 0)
        def _():
            pass_on(GM, gmb)

        @pl.when(el == 0)
        def _():
            arrive(GM, gmb, k)

        rows = pl.ds(pl.multiple_of(k * CAP, CAP), CAP)
        e = pl.ds(me * E_LOC + el, 1)
        key = keys[0, k, e, :]
        gout[el, rows] = (dot(onehot(key), gmb[k]) * gate_column(key, gates[0, k, e, :])).astype(BF)
        expert_backward(k, el, lambda n: ab1[el, n, rows], vgu1, vw1, GR_ONE, grt1)
        return carry

    lax.fori_loop(0, EP * E_LOC, backward_one, 0)
    weight_grads(0, x1, 0)
    weight_grads(0, x1, 1)
    send_weight_grads(0)
    grad_mixed = backward_combine(GR_ONE, grt1, gmb[0])
    dense_grad(0, xin[0], grad_mixed)
    dx_out[...] = grad_input(grad_mixed, vm1)

    for k in range(1, EP):
        tell(k).wait_send()
        for phase, buf in ((O_ONE, oret), (GR_TWO, grt2), (GR_ONE, grt1)):
            for el in range(E_LOC):
                giveback(phase, buf, k, el).wait_send()
    for phase, buf in ((X_IN, xin), (DY, dyb), (Y_ONE, yb), (GM, gmb)):
        for k in (1, 2):
            for piece in range(2):
                ship(phase, buf, k, piece).wait_send()
            relay(phase, buf, k).wait_send()
    for l in range(2):
        for copy in pairs(l) + dense_copies(l):
            copy.wait()


def finish(dx, wg, wu, wd, got_g, got_u, got_w, dpart, dense_got,
           dx_out, gd1, gg1, gu1, gw1, gd2, gg2, gu2, gw2,
           vg, vu, vw, vsum, out_sem):
    dp = lax.axis_index('dp')
    flat = dp * EP + lax.axis_index('ep')
    stores = []

    def store(src, dst):
        copy = pltpu.make_async_copy(src, dst, out_sem.at[len(stores)])
        copy.start()
        stores.append(copy)

    store(dx, dx_out)
    for l, outs in enumerate(((gg1, gu1, gw1), (gg2, gu2, gw2))):
        for own, got, total, out in zip((wg, wu, wd), (got_g, got_u, got_w), (vg, vu, vw), outs):
            total[l] = (own[l, dp].astype(F32) + got[l].astype(F32)).astype(BF)
            store(total.at[l], out)
    for l, out in enumerate((gd1, gd2)):
        total = dpart[l, flat].astype(F32)
        for r in range(1, EP * DP):
            total += dense_got[l, r].astype(F32)
        vsum[l] = total.astype(BF)
        store(vsum.at[l], out)
    for copy in stores:
        copy.wait()


def solution(mesh):
    tok_spec = P(('dp', 'ep'), None)
    exp_spec = P('ep', None, None)
    layer_specs = (P(None, None), tok_spec, tok_spec, exp_spec, exp_spec, exp_spec)
    grad_specs = (P(('dp', 'ep'), None), P('ep', 'dp', None), P('ep', 'dp', None), P('ep', None, 'dp'))

    def local_step(tokens, dy_out, dense_w1, route_idx1, route_gate1, w_gate1, w_up1, w_down1, dense_w2, route_idx2, route_gate2, w_gate2, w_up2, w_down2):
        hbm = pl.BlockSpec(memory_space=pl.ANY)
        half = D // DP

        def sds(*shape):
            return jax.ShapeDtypeStruct(shape, BF)

        grads = (sds(32, D), sds(E_LOC, half, FF), sds(E_LOC, half, FF), sds(E_LOC, FF, half))
        vm = pltpu.VMEM
        got = (vm((2, E_LOC, half, FF), BF), vm((2, E_LOC, half, FF), BF), vm((2, E_LOC, FF, half), BF))
        parts = (vm((2, DP, E_LOC, half, FF), BF), vm((2, DP, E_LOC, half, FF), BF), vm((2, DP, E_LOC, FF, half), BF))
        dense = vm((2, EP * DP, 32, D), BF)
        on_chip = pl.BlockSpec(memory_space=pltpu.VMEM)
        dma = pltpu.SemaphoreType.DMA
        weights = [vm((D, D), BF), vm((E_LOC, TILES, D, 2 * LANES), BF), vm((E_LOC, FF, D), BF)]
        spread_buf = vm((EP, TOK, D), BF)
        ret_buf = vm((2 * EP - 1, TOK, D), BF)
        scratch = [vm((2, 2, TOK), jnp.int32), vm((2, 2, TOK), F32)]
        scratch += [vm((EP, 8, TOK), F32), spread_buf, spread_buf, spread_buf, spread_buf, ret_buf, ret_buf, ret_buf]
        scratch += weights + weights
        scratch += [vm((TOK, TOK), BF), vm((2, EP, 8, TOK), jnp.int32), vm((2, EP, 8, TOK), F32), vm((2, 8, TOK), jnp.int32)]
        scratch += [vm((2, TOK, EP * TOK), BF)]
        scratch += [vm((E_LOC, EP * CAP, D), BF)] * 3
        scratch += [vm((E_LOC, TILES, EP * CAP, 2 * LANES), F32), vm((E_LOC, EP * CAP, FF), BF), vm((E_LOC, TILES, EP * CAP, 2 * LANES), BF)]
        scratch += [spread_buf, vm((TOK, D), F32), vm((TOK, D), F32)]
        scratch += [dma((6 + 4 * (TILES + 1),)), dma((EP,)), dma((EP,)), dma((4, EP, 2)), dma((4, EP, 2)), dma((3, EP, 2)), dma((3, EP, 2)),
                    dma((2, 3)), dma((2, 3)), dma((2, 8)), dma((2, 8))]
        results = pl.pallas_call(
            kernel,
            out_shape=(vm((TOK, D), BF),) + parts + got + (dense, dense),
            in_specs=[hbm] * 14,
            out_specs=(on_chip,) * 9,
            scratch_shapes=scratch,
            name='moe_backward',
            compiler_params=pltpu.CompilerParams(collective_id=0, has_side_effects=True, vmem_limit_bytes=VMEM_LIMIT),
        )(tokens, dy_out, route_idx1.T, route_idx2.T, route_gate1.T, route_gate2.T,
          dense_w1, w_gate1, w_up1, w_down1, dense_w2, w_gate2, w_up2, w_down2)
        return pl.pallas_call(
            finish,
            out_shape=(sds(TOK, D),) + grads + grads,
            in_specs=[on_chip] * 9,
            out_specs=(hbm,) * 9,
            scratch_shapes=list(got) + [vm((2, 32, D), BF), dma((9,))],
            name='finish',
            compiler_params=pltpu.CompilerParams(vmem_limit_bytes=16 * 1024 * 1024),
        )(*[pltpu.with_memory_space_constraint(r, pltpu.VMEM) for r in results])

    return jax.shard_map(local_step, mesh=mesh, in_specs=(tok_spec, tok_spec) + layer_specs + layer_specs,
                         out_specs=(tok_spec,) + grad_specs + grad_specs, check_vma=False)
```

time: 91.2 us -> 86.7 us (0.951)
  Pallas kernels: 90.4 us -> 85.8 us
    pallas_call x1, Pallas kernels: 4.45 us -> 1.72 us  [local_step(): pl.pallas_call(finish, out_shape=(sds(TOK, D),) + grads + grads, in_specs...]
    pallas_call x1, Pallas kernels: 85.9 us -> 84.1 us  [local_step(): pl.pallas_call(kernel, out_shape=(vm((TOK, D), BF),) + parts + got + (den...]
where the time goes in v2:
time: 86.7 us; the launch traced here: 86.6 us
  Pallas kernels  85.8 us (99%)
    pallas_call x1, Pallas kernels, local_step(): pl.pallas_call(kernel, out_shape=(vm((TOK, D), BF),) + parts + got + (den...  84.1 us

profile of v2, /device:TPU:0, one launch (start us, length us, event | category | flops | bytes accessed | tf_op | source)
XLA Modules:
  0.0 86.6 jit_solution(5255468211925664422)
XLA Ops:
  0.6 84.1 %moe_backward.1 = (bf16[512,256]{1,0:T(8,128)(2,1)S(1)}, bf16[2,2,2,128,896]{4,3,2,1,0:T(8,128)(2,1)S(1)}, bf16[2,2,2,128,896]{4,3,2,1,0:T(8,128)(2,1)S(1)}, bf1...) custom-call(bf16[512,256]{1,0:T(8,128)(2,1)} %tokens.1, ...), custom_call_target="tpu_custom_call" | custom-call | tf_op jit(solution)/shard_map/moe_backward/pallas_call | solution.py:476
  84.7 1.7 %finish.1 = (bf16[512,256]{1,0:T(8,128)(2,1)}, bf16[32,256]{1,0:T(8,128)(2,1)}, bf16[2,128,896]{2,1,0:T(8,128)(2,1)}, bf16[2,128,896]{2,1,0:T(8,128)(2,1)}, bf16...) custom-call(bf16[512,256]{1,0:T(8,128)(2,1)S(1)} %get-tuple-element., ...), custom_call_target="tpu_custom_call" | custom-call | tf_op jit(solution)/shard_map/finish/pallas_call | solution.py:486

commit v3 on v2

--- a/solution.py
+++ b/solution.py
@@ -68,25 +68,30 @@
     def partner(k):
         return (me // 2 + k // 2) % 2 * 2 + (me + k) % 2
 
-    def weight_loads(m, g, u, w, vm, vgu, vw):
-        pieces = [(m, vm), (w, vw)]
+    small = [(idx1, ibuf.at[0]), (idx2, ibuf.at[1]), (gate1, gbuf.at[0]), (gate2, gbuf.at[1]), (tokens, xin.at[0]), (dy, dyb.at[0])]
+    small = [pltpu.make_async_copy(src, dst, loc_sem.at[n]) for n, (src, dst) in enumerate(small)]
+    for copy in small:
+        copy.start()
+
+    def weight_copies(l, m, g, u, w, vm, vgu, vw):
+        base = len(small) + 3 * l
+        copies = [pltpu.make_async_copy(m, vm, loc_sem.at[base]), pltpu.make_async_copy(w, vw, loc_sem.at[base + 1])]
         for n in range(TILES):
             cols = pl.ds(n * LANES, LANES)
-            pieces += [(g.at[:, :, cols], vgu.at[:, n, :, pl.ds(0, LANES)]), (u.at[:, :, cols], vgu.at[:, n, :, pl.ds(LANES, LANES)])]
-        return pieces
-
-    loads = [(idx1, ibuf.at[0]), (idx2, ibuf.at[1]), (gate1, gbuf.at[0]), (gate2, gbuf.at[1]), (tokens, xin.at[0]), (dy, dyb.at[0])]
-    loads += weight_loads(m1, g1, u1, w1, vm1, vgu1, vw1)
-    loads_one = len(loads)
-    loads += weight_loads(m2, g2, u2, w2, vm2, vgu2, vw2)
-    loads = [pltpu.make_async_copy(src, dst, loc_sem.at[n]) for n, (src, dst) in enumerate(loads)]
-    for copy in loads:
+            for src, lanes in ((g, pl.ds(0, LANES)), (u, pl.ds(LANES, LANES))):
+                copies.append(pltpu.make_async_copy(src.at[:, :, cols], vgu.at[:, n, :, lanes], loc_sem.at[base + 2]))
+        whole = pltpu.make_async_copy(vgu, vgu, loc_sem.at[base + 2])
+        return copies, copies[:2] + [whole]
+
+    starts_one, waits_one = weight_copies(0, m1, g1, u1, w1, vm1, vgu1, vw1)
+    starts_two, waits_two = weight_copies(1, m2, g2, u2, w2, vm2, vgu2, vw2)
+    for copy in starts_one:
         copy.start()
 
-    for copy in loads[:4]:
+    for copy in small[:4]:
         copy.wait()
     rt[0] = jnp.concatenate([ibuf[0].astype(F32), ibuf[1].astype(F32), gbuf[0], gbuf[1]], axis=0)
-    loads[4].wait()
+    small[4].wait()
     pl.semaphore_wait(barrier, EP * DP - 1)
 
     def remote(src, dst, send, recv, k):
@@ -94,18 +99,24 @@
                                             device_id={'ep': partner(k)}, device_id_type=MESH)
 
     def tell(k):
-        return remote(rt.at[0], rt.at[k], rt_send.at[k], rt_recv.at[k], k)
+        return remote(rt.at[0], rt.at[k], rt_send, rt_recv.at[k - 1], k)
+
+    def lane(phase):
+        return 1 if phase == DY else 0
+
+    def all_sent(buf, sem):
+        remote(buf.at[pl.ds(1, EP - 1)], buf.at[pl.ds(1, EP - 1)], sem, sem, 1).wait_send()
 
     def half(h):
         return pl.ds(h * CAP, CAP)
 
     def ship(phase, buf, k, piece):
         rows = half(piece if k == 1 else 1 - piece)
-        return remote(buf.at[0, rows], buf.at[k, rows], ag_send.at[phase, k, piece], ag_recv.at[phase, k, piece], k)
+        return remote(buf.at[0, rows], buf.at[k, rows], ag_send.at[lane(phase)], ag_recv.at[lane(phase), k - 1, piece], k)
 
     def relay(phase, buf, via):
         rows = half(via - 1)
-        return remote(buf.at[via, rows], buf.at[3, rows], ag_send.at[phase, 3, via - 1], ag_recv.at[phase, 3, via - 1], 3 - via)
+        return remote(buf.at[via, rows], buf.at[3, rows], ag_send.at[lane(phase)], ag_recv.at[lane(phase), 2, via - 1], 3 - via)
 
     def spread(phase, buf):
         for piece in range(2):
@@ -130,17 +141,19 @@
 
     def giveback(phase, buf, k, el):
         rows = pl.ds(pl.multiple_of(el * CAP, CAP), CAP)
-        return remote(buf.at[k, rows], buf.at[k + 3, rows], ret_send.at[phase, k, el], ret_recv.at[phase, k, el], k)
+        return remote(buf.at[k, rows], buf.at[k + 3, rows], ret_send, ret_recv.at[k - 1, el], k)
 
     for k in range(1, EP):
         tell(k).start()
 
     @pl.when(dp == 1)
     def _():
-        loads[5].wait()
+        small[5].wait()
         spread(DY, dyb)
 
     spread(X_IN, xin)
+    for copy in starts_two:
+        copy.start()
 
     tri[...] = jnp.where(lax.broadcasted_iota(jnp.int32, (TOK, TOK), 0) < lax.broadcasted_iota(jnp.int32, (TOK, TOK), 1), 1.0, 0.0).astype(BF)
     expert = lax.broadcasted_iota(jnp.int32, (E_LOC * EP, TOK), 0).astype(F32)
@@ -159,7 +172,7 @@
     info = make_keys(0)
     for j in range(2):
         keyj[j] = jnp.where(info[j:j + 1] == expert, keys[0, 0], -1)
-    for copy in loads[6:loads_one]:
+    for copy in waits_one:
         copy.wait()
 
     def build_picks(*sources):
@@ -231,10 +244,10 @@
 
     @pl.when(dp == 0)
     def _():
-        loads[5].wait()
+        small[5].wait()
         spread(DY, dyb)
 
-    for copy in loads[loads_one:]:
+    for copy in waits_two:
         copy.wait()
 
     def collect(phase, ret, ks):
@@ -251,6 +264,7 @@
     out0 = p0[...] + picked(0, oret, True)
     out1 = p1[...] + picked(1, oret, True)
     yb[0] = (ub[0].astype(F32) + (gcol0 * out0 + gcol1 * out1)).astype(BF)
+    all_sent(xin, ag_send.at[0])
     spread(Y_ONE, yb)
 
     def expert_backward(k, el, first, vgu, vw, phase, ret):
@@ -277,6 +291,8 @@
         def _():
             giveback(phase, ret, k, el).start()
 
+    all_sent(oret, ret_send)
+
     def layer_two(i, carry):
         k, el = unit(i)
 
@@ -311,7 +327,7 @@
     stacks = ((wg, got_g), (wu, got_u), (wd, got_w))
 
     def pairs(l):
-        return [pltpu.make_async_remote_copy(src_ref=part.at[l, other], dst_ref=got.at[l], send_sem=dp_send.at[l, n],
+        return [pltpu.make_async_remote_copy(src_ref=part.at[l, other], dst_ref=got.at[l], send_sem=dp_send.at[n],
                                              recv_sem=dp_recv.at[l, n], device_id={'dp': other}, device_id_type=MESH)
                 for n, (part, got) in enumerate(stacks)]
 
@@ -331,6 +347,9 @@
                 wu[l, d, el, :, cols] = both[rows, LANES:]
 
     def send_weight_grads(l):
+        if l == 0:
+            for copy in pairs(1):
+                copy.wait_send()
         for copy in pairs(l):
             copy.start()
 
@@ -350,7 +369,7 @@
         for r in range(1, EP * DP):
             peer = (flat + r) % (EP * DP)
             copies.append(pltpu.make_async_remote_copy(
-                src_ref=dpart.at[l, peer], dst_ref=dense_got.at[l, r], send_sem=all_send.at[l, r], recv_sem=all_recv.at[l, r],
+                src_ref=dpart.at[l, peer], dst_ref=dense_got.at[l, r], send_sem=all_send.at[l], recv_sem=all_recv.at[l],
                 device_id={'ep': peer % EP, 'dp': peer // EP}, device_id_type=MESH))
         return copies
 
@@ -363,11 +382,14 @@
 
     grad_mixed = backward_combine(GR_TWO, grt2, dyb[0])
     gmb[0] = grad_input(grad_mixed, vm2)
+    all_sent(yb, ag_send.at[0])
     spread(GM, gmb)
     weight_grads(1, x2, 1)
     send_weight_grads(1)
     dense_grad(1, yb[0], grad_mixed)
 
+    all_sent(grt2, ret_send)
+
     def backward_one(i, carry):
         k, el = unit(i)
 
@@ -375,7 +397,7 @@
         def _():
             build_picks(keys.at[0, 0])
 
-        @pl.when(i == 0)
+        @pl.when(i == 1)
         def _():
             pass_on(GM, gmb)
 
@@ -398,19 +420,18 @@
     dense_grad(0, xin[0], grad_mixed)
     dx_out[...] = grad_input(grad_mixed, vm1)
 
-    for k in range(1, EP):
-        tell(k).wait_send()
-        for phase, buf in ((O_ONE, oret), (GR_TWO, grt2), (GR_ONE, grt1)):
-            for el in range(E_LOC):
-                giveback(phase, buf, k, el).wait_send()
-    for phase, buf in ((X_IN, xin), (DY, dyb), (Y_ONE, yb), (GM, gmb)):
-        for k in (1, 2):
-            for piece in range(2):
-                ship(phase, buf, k, piece).wait_send()
-            relay(phase, buf, k).wait_send()
+    all_sent(rt, rt_send)
+    all_sent(dyb, ag_send.at[1])
+    all_sent(gmb, ag_send.at[0])
+    all_sent(grt1, ret_send)
+    for copy in pairs(1):
+        copy.wait_recv()
+    for copy in pairs(0):
+        copy.wait()
     for l in range(2):
-        for copy in pairs(l) + dense_copies(l):
-            copy.wait()
+        whole = pl.ds(1, EP * DP - 1)
+        pltpu.make_async_remote_copy(src_ref=dpart.at[l, whole], dst_ref=dense_got.at[l, whole], send_sem=all_send.at[l], recv_sem=all_recv.at[l],
+                                     device_id={'dp': other}, device_id_type=MESH).wait()
 
 
 def finish(dx, wg, wu, wd, got_g, got_u, got_w, dpart, dense_got,
@@ -471,8 +492,8 @@
         scratch += [vm((E_LOC, EP * CAP, D), BF)] * 3
         scratch += [vm((E_LOC, TILES, EP * CAP, 2 * LANES), F32), vm((E_LOC, EP * CAP, FF), BF), vm((E_LOC, TILES, EP * CAP, 2 * LANES), BF)]
         scratch += [spread_buf, vm((TOK, D), F32), vm((TOK, D), F32)]
-        scratch += [dma((6 + 4 * (TILES + 1),)), dma((EP,)), dma((EP,)), dma((4, EP, 2)), dma((4, EP, 2)), dma((3, EP, 2)), dma((3, EP, 2)),
-                    dma((2, 3)), dma((2, 3)), dma((2, 8)), dma((2, 8))]
+        scratch += [dma((12,)), dma, dma((EP - 1,)), dma((2,)), dma((2, EP - 1, 2)), dma, dma((EP - 1, 2)),
+                    dma((3,)), dma((2, 3)), dma((2,)), dma((2,))]
         results = pl.pallas_call(
             kernel,
             out_shape=(vm((TOK, D), BF),) + parts + got + (dense, dense),

time: 86.7 us -> 84.4 us (0.973)
  Pallas kernels: 85.8 us -> 83.5 us
    pallas_call x1, Pallas kernels: 84.1 us -> 81.8 us  [local_step(): pl.pallas_call(kernel, out_shape=(vm((TOK, D), BF),) + parts + got + (den...]
where the time goes in v3:
time: 84.4 us; the launch traced here: 84.3 us
  Pallas kernels  83.5 us (99%)
    pallas_call x1, Pallas kernels, local_step(): pl.pallas_call(kernel, out_shape=(vm((TOK, D), BF),) + parts + got + (den...  81.8 us
    pallas_call x1, Pallas kernels, local_step(): pl.pallas_call(finish, out_shape=(sds(TOK, D),) + grads + grads, in_specs...  1.72 us

profile of v3, /device:TPU:0, one launch (start us, length us, event | category | flops | bytes accessed | tf_op | source)
XLA Modules:
  0.0 84.3 jit_solution(15797117743825113317)
XLA Ops:
  0.6 81.8 %moe_backward.1 = (bf16[512,256]{1,0:T(8,128)(2,1)S(1)}, bf16[2,2,2,128,896]{4,3,2,1,0:T(8,128)(2,1)S(1)}, bf16[2,2,2,128,896]{4,3,2,1,0:T(8,128)(2,1)S(1)}, bf1...) custom-call(bf16[512,256]{1,0:T(8,128)(2,1)} %tokens.1, ...), custom_call_target="tpu_custom_call" | custom-call | tf_op jit(solution)/shard_map/moe_backward/pallas_call | solution.py:497
  82.4 1.7 %finish.1 = (bf16[512,256]{1,0:T(8,128)(2,1)}, bf16[32,256]{1,0:T(8,128)(2,1)}, bf16[2,128,896]{2,1,0:T(8,128)(2,1)}, bf16[2,128,896]{2,1,0:T(8,128)(2,1)}, bf16...) custom-call(bf16[512,256]{1,0:T(8,128)(2,1)S(1)} %get-tuple-element., ...), custom_call_target="tpu_custom_call" | custom-call | tf_op jit(solution)/shard_map/finish/pallas_call | solution.py:507

commit v4 on v3

--- a/solution.py
+++ b/solution.py
@@ -20,7 +20,7 @@
 FF = 896
 LANES = 128
 TILES = FF // LANES
-VMEM_LIMIT = 54 * 1024 * 1024
+VMEM_LIMIT = 60 * 1024 * 1024
 X_IN, DY, Y_ONE, GM = range(4)
 O_ONE, GR_TWO, GR_ONE = range(3)
 
@@ -50,10 +50,11 @@
 
 
 def kernel(tokens, dy, idx1, idx2, gate1, gate2, m1, g1, u1, w1, m2, g2, u2, w2,
-           dx_out, wg, wu, wd, got_g, got_u, got_w, dpart, dense_got,
+           dx_out, got_g, got_u, got_w, dense_sum,
            ibuf, gbuf, rt, xin, dyb, yb, gmb, oret, grt2, grt1,
            vm1, vgu1, vw1, vm2, vgu2, vw2,
            tri, keys, gates, keyj, picks, x1, x2, gout, ab1, hb, gab, ub, p0, p1,
+           wg, wu, wd, dpart, dense_got,
            loc_sem, rt_send, rt_recv, ag_send, ag_recv, ret_send, ret_recv, dp_send, dp_recv, all_send, all_recv):
     me = lax.axis_index('ep')
     dp = lax.axis_index('dp')
@@ -61,12 +62,12 @@
     other = 1 - dp
 
     barrier = pltpu.get_barrier_semaphore()
-    for r in range(1, EP * DP):
-        peer = (flat + r) % (EP * DP)
-        pl.semaphore_signal(barrier, inc=1, device_id={'ep': peer % EP, 'dp': peer // EP}, device_id_type=MESH)
-
     def partner(k):
         return (me // 2 + k // 2) % 2 * 2 + (me + k) % 2
+
+    for k in (1, 2):
+        pl.semaphore_signal(barrier, inc=1, device_id={'ep': partner(k)}, device_id_type=MESH)
+    pl.semaphore_signal(barrier, inc=1, device_id={'dp': other}, device_id_type=MESH)
 
     small = [(idx1, ibuf.at[0]), (idx2, ibuf.at[1]), (gate1, gbuf.at[0]), (gate2, gbuf.at[1]), (tokens, xin.at[0]), (dy, dyb.at[0])]
     small = [pltpu.make_async_copy(src, dst, loc_sem.at[n]) for n, (src, dst) in enumerate(small)]
@@ -92,7 +93,7 @@
         copy.wait()
     rt[0] = jnp.concatenate([ibuf[0].astype(F32), ibuf[1].astype(F32), gbuf[0], gbuf[1]], axis=0)
     small[4].wait()
-    pl.semaphore_wait(barrier, EP * DP - 1)
+    pl.semaphore_wait(barrier, 3)
 
     def remote(src, dst, send, recv, k):
         return pltpu.make_async_remote_copy(src_ref=src, dst_ref=dst, send_sem=send, recv_sem=recv,
@@ -129,13 +130,9 @@
             relay(phase, buf, via).start()
 
     def arrive(phase, buf, k):
-        for near in (1, 2):
-            @pl.when(k == near)
-            def _():
-                ship(phase, buf, near, 1).wait_recv()
-
-        @pl.when(k == 3)
-        def _():
+        if k < 3:
+            ship(phase, buf, k, 1).wait_recv()
+        else:
             for via in (1, 2):
                 relay(phase, buf, via).wait_recv()
 
@@ -143,7 +140,7 @@
         rows = pl.ds(pl.multiple_of(el * CAP, CAP), CAP)
         return remote(buf.at[k, rows], buf.at[k + 3, rows], ret_send, ret_recv.at[k - 1, el], k)
 
-    for k in range(1, EP):
+    for k in (1, 2):
         tell(k).start()
 
     @pl.when(dp == 1)
@@ -198,10 +195,15 @@
     def mixed(x, m):
         return (x.astype(F32) + dot(x, m[...])).astype(BF)
 
-    def forward_one(i, carry):
-        k, el = unit(i)
-
-        @pl.when(i == 2)
+    def near_or_far(b):
+        return ((b == 1, 1), (b == 1, 2), (b == 3, 3))
+
+    def forward_one(b, carry):
+        @pl.when(b == 0)
+        def _():
+            ub[0] = mixed(xin[0], vm1)
+
+        @pl.when(b == 1)
         def _():
             build_picks(keyj.at[0], keyj.at[1])
 
@@ -209,38 +211,44 @@
             def _():
                 pass_on(DY, dyb)
 
+            tell(1).wait_recv()
+            remote(rt.at[1], rt.at[3], rt_send, rt_recv.at[2], 2).start()
             pass_on(X_IN, xin)
 
-        @pl.when(el == 0)
+        for ready, src in near_or_far(b):
+            @pl.when(ready)
+            def _():
+                if src > 1:
+                    tell(src).wait_recv()
+                make_keys(src)
+                arrive(X_IN, xin, src)
+                ub[src] = mixed(xin[src], vm1)
+
+        for k, el in (unit(2 * b), unit(2 * b + 1)):
+            rows = pl.ds(pl.multiple_of(k * CAP, CAP), CAP)
+            key = keys[0, k, pl.ds(me * E_LOC + el, 1), :]
+            x = dot(onehot(key), ub[k]).astype(BF)
+            x1[el, rows] = x
+            out = jnp.zeros((CAP, D), F32)
+            for group in groups():
+                h = []
+                for n in group:
+                    ab = dot(x, vgu1[el, n])
+                    ab1[el, n, rows] = ab
+                    h.append((silu_parts(ab[:, :LANES])[1] * ab[:, LANES:]).astype(BF))
+                out += dot(jnp.concatenate(h, axis=1), vw1[el, group[0] * LANES:(group[-1] + 1) * LANES])
+            oret[k, pl.ds(pl.multiple_of(el * CAP, CAP), CAP)] = out.astype(BF)
+
+        returns(b, O_ONE, oret)
+        return carry
+
+    def returns(b, phase, ret):
+        @pl.when(b > 0)
         def _():
-            @pl.when(k > 0)
-            def _():
-                tell(k).wait_recv()
-                make_keys(k)
-
-            arrive(X_IN, xin, k)
-            ub[k] = mixed(xin[k], vm1)
-
-        rows = pl.ds(pl.multiple_of(k * CAP, CAP), CAP)
-        key = keys[0, k, pl.ds(me * E_LOC + el, 1), :]
-        x = dot(onehot(key), ub[k]).astype(BF)
-        x1[el, rows] = x
-        out = jnp.zeros((CAP, D), F32)
-        for group in groups():
-            h = []
-            for n in group:
-                ab = dot(x, vgu1[el, n])
-                ab1[el, n, rows] = ab
-                h.append((silu_parts(ab[:, :LANES])[1] * ab[:, LANES:]).astype(BF))
-            out += dot(jnp.concatenate(h, axis=1), vw1[el, group[0] * LANES:(group[-1] + 1) * LANES])
-        oret[k, pl.ds(pl.multiple_of(el * CAP, CAP), CAP)] = out.astype(BF)
-
-        @pl.when(k > 0)
-        def _():
-            giveback(O_ONE, oret, k, el).start()
-        return carry
-
-    lax.fori_loop(0, EP * E_LOC, forward_one, 0)
+            for k, el in (unit(2 * b), unit(2 * b + 1)):
+                giveback(phase, ret, k, el).start()
+
+    lax.fori_loop(0, EP, forward_one, 0)
 
     @pl.when(dp == 0)
     def _():
@@ -267,7 +275,7 @@
     all_sent(xin, ag_send.at[0])
     spread(Y_ONE, yb)
 
-    def expert_backward(k, el, first, vgu, vw, phase, ret):
+    def expert_backward(k, el, first, vgu, vw, ret):
         rows = pl.ds(pl.multiple_of(k * CAP, CAP), CAP)
         go = gout[el, rows]
         back = jnp.zeros((CAP, D), F32)
@@ -287,16 +295,14 @@
                 back += dot(grads, vgu[el, n], NT)
         ret[k, pl.ds(pl.multiple_of(el * CAP, CAP), CAP)] = back.astype(BF)
 
-        @pl.when(k > 0)
+    all_sent(oret, ret_send)
+
+    def layer_two(b, carry):
+        @pl.when(b == 0)
         def _():
-            giveback(phase, ret, k, el).start()
-
-    all_sent(oret, ret_send)
-
-    def layer_two(i, carry):
-        k, el = unit(i)
-
-        @pl.when(i == 2)
+            ub[0] = mixed(yb[0], vm2)
+
+        @pl.when(b == 1)
         def _():
             build_picks(keys.at[1, 0])
 
@@ -306,23 +312,27 @@
 
             pass_on(Y_ONE, yb)
 
-        @pl.when(el == 0)
-        def _():
-            arrive(DY, dyb, k)
-            arrive(Y_ONE, yb, k)
-            ub[k] = mixed(yb[k], vm2)
-
-        rows = pl.ds(pl.multiple_of(k * CAP, CAP), CAP)
-        e = pl.ds(me * E_LOC + el, 1)
-        key = keys[1, k, e, :]
-        pick = onehot(key)
-        x = dot(pick, ub[k]).astype(BF)
-        x2[el, rows] = x
-        gout[el, rows] = (dot(pick, dyb[k]) * gate_column(key, gates[1, k, e, :])).astype(BF)
-        expert_backward(k, el, lambda n: dot(x, vgu2[el, n]), vgu2, vw2, GR_TWO, grt2)
+        for ready, src in near_or_far(b):
+            @pl.when(ready)
+            def _():
+                arrive(DY, dyb, src)
+                arrive(Y_ONE, yb, src)
+                ub[src] = mixed(yb[src], vm2)
+
+        for k, el in (unit(2 * b), unit(2 * b + 1)):
+            rows = pl.ds(pl.multiple_of(k * CAP, CAP), CAP)
+            e = pl.ds(me * E_LOC + el, 1)
+            key = keys[1, k, e, :]
+            pick = onehot(key)
+            x = dot(pick, ub[k]).astype(BF)
+            x2[el, rows] = x
+            gout[el, rows] = (dot(pick, dyb[k]) * gate_column(key, gates[1, k, e, :])).astype(BF)
+            expert_backward(k, el, lambda n: dot(x, vgu2[el, n]), vgu2, vw2, grt2)
+
+        returns(b, GR_TWO, grt2)
         return carry
 
-    lax.fori_loop(0, EP * E_LOC, layer_two, 0)
+    lax.fori_loop(0, EP, layer_two, 0)
 
     stacks = ((wg, got_g), (wu, got_u), (wd, got_w))
 
@@ -390,29 +400,28 @@
 
     all_sent(grt2, ret_send)
 
-    def backward_one(i, carry):
-        k, el = unit(i)
-
-        @pl.when(i == 2)
+    def backward_one(b, carry):
+        @pl.when(b == 0)
         def _():
             build_picks(keys.at[0, 0])
-
-        @pl.when(i == 1)
-        def _():
             pass_on(GM, gmb)
 
-        @pl.when(el == 0)
-        def _():
-            arrive(GM, gmb, k)
-
-        rows = pl.ds(pl.multiple_of(k * CAP, CAP), CAP)
-        e = pl.ds(me * E_LOC + el, 1)
-        key = keys[0, k, e, :]
-        gout[el, rows] = (dot(onehot(key), gmb[k]) * gate_column(key, gates[0, k, e, :])).astype(BF)
-        expert_backward(k, el, lambda n: ab1[el, n, rows], vgu1, vw1, GR_ONE, grt1)
+        for ready, src in near_or_far(b):
+            @pl.when(ready)
+            def _():
+                arrive(GM, gmb, src)
+
+        for k, el in (unit(2 * b), unit(2 * b + 1)):
+            rows = pl.ds(pl.multiple_of(k * CAP, CAP), CAP)
+            e = pl.ds(me * E_LOC + el, 1)
+            key = keys[0, k, e, :]
+            gout[el, rows] = (dot(onehot(key), gmb[k]) * gate_column(key, gates[0, k, e, :])).astype(BF)
+            expert_backward(k, el, lambda n: ab1[el, n, rows], vgu1, vw1, grt1)
+
+        returns(b, GR_ONE, grt1)
         return carry
 
-    lax.fori_loop(0, EP * E_LOC, backward_one, 0)
+    lax.fori_loop(0, EP, backward_one, 0)
     weight_grads(0, x1, 0)
     weight_grads(0, x1, 1)
     send_weight_grads(0)
@@ -429,35 +438,25 @@
     for copy in pairs(0):
         copy.wait()
     for l in range(2):
+        for part, got in stacks:
+            got[l] = (part[l, dp].astype(F32) + got[l].astype(F32)).astype(BF)
+    for l in range(2):
         whole = pl.ds(1, EP * DP - 1)
         pltpu.make_async_remote_copy(src_ref=dpart.at[l, whole], dst_ref=dense_got.at[l, whole], send_sem=all_send.at[l], recv_sem=all_recv.at[l],
                                      device_id={'dp': other}, device_id_type=MESH).wait()
-
-
-def finish(dx, wg, wu, wd, got_g, got_u, got_w, dpart, dense_got,
-           dx_out, gd1, gg1, gu1, gw1, gd2, gg2, gu2, gw2,
-           vg, vu, vw, vsum, out_sem):
-    dp = lax.axis_index('dp')
-    flat = dp * EP + lax.axis_index('ep')
-    stores = []
-
-    def store(src, dst):
-        copy = pltpu.make_async_copy(src, dst, out_sem.at[len(stores)])
-        copy.start()
-        stores.append(copy)
-
-    store(dx, dx_out)
-    for l, outs in enumerate(((gg1, gu1, gw1), (gg2, gu2, gw2))):
-        for own, got, total, out in zip((wg, wu, wd), (got_g, got_u, got_w), (vg, vu, vw), outs):
-            total[l] = (own[l, dp].astype(F32) + got[l].astype(F32)).astype(BF)
-            store(total.at[l], out)
-    for l, out in enumerate((gd1, gd2)):
         total = dpart[l, flat].astype(F32)
         for r in range(1, EP * DP):
             total += dense_got[l, r].astype(F32)
-        vsum[l] = total.astype(BF)
-        store(vsum.at[l], out)
-    for copy in stores:
+        dense_sum[l] = total.astype(BF)
+
+
+def finish(dx, got_g, got_u, got_w, dense_sum, dx_out, gd1, gg1, gu1, gw1, gd2, gg2, gu2, gw2, out_sem):
+    moves = [(got_g.at[0], gg1), (got_u.at[0], gu1), (got_w.at[0], gw1), (got_g.at[1], gg2), (got_u.at[1], gu2), (got_w.at[1], gw2),
+             (dx, dx_out), (dense_sum.at[0], gd1), (dense_sum.at[1], gd2)]
+    moves = [pltpu.make_async_copy(src, dst, out_sem.at[n]) for n, (src, dst) in enumerate(moves)]
+    for copy in moves:
+        copy.start()
+    for copy in moves:
         copy.wait()
 
 
@@ -492,13 +491,14 @@
         scratch += [vm((E_LOC, EP * CAP, D), BF)] * 3
         scratch += [vm((E_LOC, TILES, EP * CAP, 2 * LANES), F32), vm((E_LOC, EP * CAP, FF), BF), vm((E_LOC, TILES, EP * CAP, 2 * LANES), BF)]
         scratch += [spread_buf, vm((TOK, D), F32), vm((TOK, D), F32)]
+        scratch += list(parts) + [dense, dense]
         scratch += [dma((12,)), dma, dma((EP - 1,)), dma((2,)), dma((2, EP - 1, 2)), dma, dma((EP - 1, 2)),
                     dma((3,)), dma((2, 3)), dma((2,)), dma((2,))]
         results = pl.pallas_call(
             kernel,
-            out_shape=(vm((TOK, D), BF),) + parts + got + (dense, dense),
+            out_shape=(vm((TOK, D), BF),) + got + (vm((2, 32, D), BF),),
             in_specs=[hbm] * 14,
-            out_specs=(on_chip,) * 9,
+            out_specs=(on_chip,) * 5,
             scratch_shapes=scratch,
             name='moe_backward',
             compiler_params=pltpu.CompilerParams(collective_id=0, has_side_effects=True, vmem_limit_bytes=VMEM_LIMIT),
@@ -507,9 +507,9 @@
         return pl.pallas_call(
             finish,
             out_shape=(sds(TOK, D),) + grads + grads,
-            in_specs=[on_chip] * 9,
+            in_specs=[on_chip] * 5,
             out_specs=(hbm,) * 9,
-            scratch_shapes=list(got) + [vm((2, 32, D), BF), dma((9,))],
+            scratch_shapes=[dma((9,))],
             name='finish',
             compiler_params=pltpu.CompilerParams(vmem_limit_bytes=16 * 1024 * 1024),
         )(*[pltpu.with_memory_space_constraint(r, pltpu.VMEM) for r in results])

time: 84.4 us -> 83.8 us (level)
  no operation moved by 1% of the time
where the time goes in v4:
time: 83.8 us; the launch traced here: 83.7 us
  Pallas kernels  82.8 us (99%)
    pallas_call x1, Pallas kernels, local_step(): pl.pallas_call(kernel, out_shape=(vm((TOK, D), BF),) + got + (vm((2, 32,...  81.1 us
    pallas_call x1, Pallas kernels, local_step(): pl.pallas_call(finish, out_shape=(sds(TOK, D),) + grads + grads, in_specs...  1.69 us

profile of v4, /device:TPU:0, one launch (start us, length us, event | category | flops | bytes accessed | tf_op | source)
XLA Modules:
  0.0 83.7 jit_solution(2585479103630848926)
XLA Ops:
  0.6 81.1 %moe_backward.1 = (bf16[512,256]{1,0:T(8,128)(2,1)S(1)}, bf16[2,2,128,896]{3,2,1,0:T(8,128)(2,1)S(1)}, bf16[2,2,128,896]{3,2,1,0:T(8,128)(2,1)S(1)}, bf16[2,2,89...) custom-call(bf16[512,256]{1,0:T(8,128)(2,1)} %tokens.1, bf16[512,256]{1,0:T(8,128)(2,1)} %dy.1, s32[2,512]{1,0:T(2,128)} %bitcast.4, ...), custom_call_target="tpu_custom_call" | custom-call | tf_op jit(solution)/shard_map/moe_backward/pallas_call | solution.py:497
  81.8 1.7 %finish.1 = (bf16[512,256]{1,0:T(8,128)(2,1)}, bf16[32,256]{1,0:T(8,128)(2,1)}, bf16[2,128,896]{2,1,0:T(8,128)(2,1)}, bf16[2,128,896]{2,1,0:T(8,128)(2,1)}, bf16...) custom-call(bf16[512,256]{1,0:T(8,128)(2,1)S(1)} %get-tuple-element., ...), custom_call_target="tpu_custom_call" | custom-call | tf_op jit(solution)/shard_map/finish/pallas_call | solution.py:507

commit v5 on v4

--- a/solution.py
+++ b/solution.py
@@ -182,7 +182,8 @@
 
     def picked(j, ret, last):
         if last:
-            return dot(picks[j, :, 3 * TOK:], ret[6])
+            rows = slice((last - 1) * CAP, last * CAP)
+            return dot(picks[j, :, 3 * TOK + (last - 1) * CAP:3 * TOK + last * CAP], ret[6, rows])
         return dot(picks[j, :, :TOK], ret[0]) + dot(picks[j, :, TOK:3 * TOK], ret[4:6].reshape(2 * TOK, D))
 
     def silu_parts(a):
@@ -258,20 +259,28 @@
     for copy in waits_two:
         copy.wait()
 
-    def collect(phase, ret, ks):
+    def collect(phase, ret, ks, els=range(E_LOC)):
         for k in ks:
-            for el in range(E_LOC):
+            for el in els:
                 giveback(phase, ret, k, el).wait_recv()
 
     collect(O_ONE, oret, (1, 2))
-    p0[...] = picked(0, oret, False)
-    p1[...] = picked(1, oret, False)
+    p0[...] = picked(0, oret, 0)
+    p1[...] = picked(1, oret, 0)
     gcol0 = jnp.transpose(jnp.broadcast_to(rt[0, 4:5], (8, TOK)))[:, :1]
     gcol1 = jnp.transpose(jnp.broadcast_to(rt[0, 5:6], (8, TOK)))[:, :1]
-    collect(O_ONE, oret, (3,))
-    out0 = p0[...] + picked(0, oret, True)
-    out1 = p1[...] + picked(1, oret, True)
+    collect(O_ONE, oret, (3,), (0,))
+    p0[...] += picked(0, oret, 1)
+    p1[...] += picked(1, oret, 1)
+    collect(O_ONE, oret, (3,), (1,))
+    out0 = p0[...] + picked(0, oret, 2)
+    out1 = p1[...] + picked(1, oret, 2)
     yb[0] = (ub[0].astype(F32) + (gcol0 * out0 + gcol1 * out1)).astype(BF)
+    @pl.when(dp == 1)
+    def _():
+        build_picks(keys.at[1, 0])
+        ub[0] = mixed(yb[0], vm2)
+
     all_sent(xin, ag_send.at[0])
     spread(Y_ONE, yb)
 
@@ -300,11 +309,15 @@
     def layer_two(b, carry):
         @pl.when(b == 0)
         def _():
-            ub[0] = mixed(yb[0], vm2)
+            @pl.when(dp == 0)
+            def _():
+                ub[0] = mixed(yb[0], vm2)
 
         @pl.when(b == 1)
         def _():
-            build_picks(keys.at[1, 0])
+            @pl.when(dp == 0)
+            def _():
+                build_picks(keys.at[1, 0])
 
             @pl.when(dp == 0)
             def _():
@@ -367,9 +380,11 @@
 
     def backward_combine(phase, ret, grad_y):
         collect(phase, ret, (1, 2))
-        p0[...] = picked(0, ret, False)
-        collect(phase, ret, (3,))
-        return (grad_y.astype(F32) + (p0[...] + picked(0, ret, True))).astype(BF)
+        p0[...] = picked(0, ret, 0)
+        collect(phase, ret, (3,), (0,))
+        p0[...] += picked(0, ret, 1)
+        collect(phase, ret, (3,), (1,))
+        return (grad_y.astype(F32) + (p0[...] + picked(0, ret, 2))).astype(BF)
 
     def grad_input(grad_mixed, m):
         return (grad_mixed.astype(F32) + dot(grad_mixed, m[...], NT)).astype(BF)

time: 83.8 us -> 83 us (level)
  no operation moved by 1% of the time
where the time goes in v5:
time: 83 us; the launch traced here: 82.9 us
  Pallas kernels  82.1 us (99%)
  between operations  0.84 us (1%)
    pallas_call x1, Pallas kernels, local_step(): pl.pallas_call(kernel, out_shape=(vm((TOK, D), BF),) + got + (vm((2, 32,...  80.4 us
    pallas_call x1, Pallas kernels, local_step(): pl.pallas_call(finish, out_shape=(sds(TOK, D),) + grads + grads, in_specs...  1.69 us

profile of v5, /device:TPU:0, one launch (start us, length us, event | category | flops | bytes accessed | tf_op | source)
XLA Modules:
  0.0 82.9 jit_solution(9509199117197233659)
XLA Ops:
  0.6 80.4 %moe_backward.1 = (bf16[512,256]{1,0:T(8,128)(2,1)S(1)}, bf16[2,2,128,896]{3,2,1,0:T(8,128)(2,1)S(1)}, bf16[2,2,128,896]{3,2,1,0:T(8,128)(2,1)S(1)}, bf16[2,2,89...) custom-call(bf16[512,256]{1,0:T(8,128)(2,1)} %tokens.1, bf16[512,256]{1,0:T(8,128)(2,1)} %dy.1, s32[2,512]{1,0:T(2,128)} %bitcast.4, ...), custom_call_target="tpu_custom_call" | custom-call | tf_op jit(solution)/shard_map/moe_backward/pallas_call | solution.py:512
  81.0 1.7 %finish.1 = (bf16[512,256]{1,0:T(8,128)(2,1)}, bf16[32,256]{1,0:T(8,128)(2,1)}, bf16[2,128,896]{2,1,0:T(8,128)(2,1)}, bf16[2,128,896]{2,1,0:T(8,128)(2,1)}, bf16...) custom-call(bf16[512,256]{1,0:T(8,128)(2,1)S(1)} %get-tuple-element., ...), custom_call_target="tpu_custom_call" | custom-call | tf_op jit(solution)/shard_map/finish/pallas_call | solution.py:522

commit v6 on v5

--- a/solution.py
+++ b/solution.py
@@ -278,8 +278,7 @@
     yb[0] = (ub[0].astype(F32) + (gcol0 * out0 + gcol1 * out1)).astype(BF)
     @pl.when(dp == 1)
     def _():
-        build_picks(keys.at[1, 0])
-        ub[0] = mixed(yb[0], vm2)
+        pl.delay(1800)
 
     all_sent(xin, ag_send.at[0])
     spread(Y_ONE, yb)
@@ -309,15 +308,11 @@
     def layer_two(b, carry):
         @pl.when(b == 0)
         def _():
-            @pl.when(dp == 0)
-            def _():
-                ub[0] = mixed(yb[0], vm2)
+            ub[0] = mixed(yb[0], vm2)
 
         @pl.when(b == 1)
         def _():
-            @pl.when(dp == 0)
-            def _():
-                build_picks(keys.at[1, 0])
+            build_picks(keys.at[1, 0])
 
             @pl.when(dp == 0)
             def _():

time: 83 us -> 82.1 us (0.989)
  Pallas kernels: 82.1 us -> 81.1 us
    pallas_call x1, Pallas kernels: 80.4 us -> 79.4 us  [local_step(): pl.pallas_call(kernel, out_shape=(vm((TOK, D), BF),) + got + (vm((2, 32,...]
where the time goes in v6:
time: 82.1 us; the launch traced here: 81.9 us
  Pallas kernels  81.1 us (99%)
  between operations  0.84 us (1%)
    pallas_call x1, Pallas kernels, local_step(): pl.pallas_call(kernel, out_shape=(vm((TOK, D), BF),) + got + (vm((2, 32,...  79.4 us
    pallas_call x1, Pallas kernels, local_step(): pl.pallas_call(finish, out_shape=(sds(TOK, D),) + grads + grads, in_specs...  1.69 us

profile of v6, /device:TPU:0, one launch (start us, length us, event | category | flops | bytes accessed | tf_op | source)
XLA Modules:
  0.0 81.9 jit_solution(3134717461574487276)
XLA Ops:
  0.6 79.4 %moe_backward.1 = (bf16[512,256]{1,0:T(8,128)(2,1)S(1)}, bf16[2,2,128,896]{3,2,1,0:T(8,128)(2,1)S(1)}, bf16[2,2,128,896]{3,2,1,0:T(8,128)(2,1)S(1)}, bf16[2,2,89...) custom-call(bf16[512,256]{1,0:T(8,128)(2,1)} %tokens.1, bf16[512,256]{1,0:T(8,128)(2,1)} %dy.1, s32[2,512]{1,0:T(2,128)} %bitcast.4, ...), custom_call_target="tpu_custom_call" | custom-call | tf_op jit(solution)/shard_map/moe_backward/pallas_call | solution.py:507
  80.1 1.7 %finish.1 = (bf16[512,256]{1,0:T(8,128)(2,1)}, bf16[32,256]{1,0:T(8,128)(2,1)}, bf16[2,128,896]{2,1,0:T(8,128)(2,1)}, bf16[2,128,896]{2,1,0:T(8,128)(2,1)}, bf16...) custom-call(bf16[512,256]{1,0:T(8,128)(2,1)S(1)} %get-tuple-element., ...), custom_call_target="tpu_custom_call" | custom-call | tf_op jit(solution)/shard_map/finish/pallas_call | solution.py:517

commit v7 on v6

--- a/solution.py
+++ b/solution.py
@@ -184,7 +184,10 @@
         if last:
             rows = slice((last - 1) * CAP, last * CAP)
             return dot(picks[j, :, 3 * TOK + (last - 1) * CAP:3 * TOK + last * CAP], ret[6, rows])
-        return dot(picks[j, :, :TOK], ret[0]) + dot(picks[j, :, TOK:3 * TOK], ret[4:6].reshape(2 * TOK, D))
+        return dot(picks[j, :, TOK:3 * TOK], ret[4:6].reshape(2 * TOK, D))
+
+    def picked_own(j, ret):
+        return dot(picks[j, :, :TOK], ret[0])
 
     def silu_parts(a):
         sig = 0.5 * jnp.tanh(0.5 * a) + 0.5
@@ -264,9 +267,11 @@
             for el in els:
                 giveback(phase, ret, k, el).wait_recv()
 
+    p0[...] = picked_own(0, oret)
+    p1[...] = picked_own(1, oret)
     collect(O_ONE, oret, (1, 2))
-    p0[...] = picked(0, oret, 0)
-    p1[...] = picked(1, oret, 0)
+    p0[...] += picked(0, oret, 0)
+    p1[...] += picked(1, oret, 0)
     gcol0 = jnp.transpose(jnp.broadcast_to(rt[0, 4:5], (8, TOK)))[:, :1]
     gcol1 = jnp.transpose(jnp.broadcast_to(rt[0, 5:6], (8, TOK)))[:, :1]
     collect(O_ONE, oret, (3,), (0,))
@@ -374,8 +379,9 @@
     weight_grads(1, x2, 0)
 
     def backward_combine(phase, ret, grad_y):
+        p0[...] = picked_own(0, ret)
         collect(phase, ret, (1, 2))
-        p0[...] = picked(0, ret, 0)
+        p0[...] += picked(0, ret, 0)
         collect(phase, ret, (3,), (0,))
         p0[...] += picked(0, ret, 1)
         collect(phase, ret, (3,), (1,))

time: 82.1 us -> 83.3 us (1.015)
  Pallas kernels: 81.1 us -> 82.4 us
    pallas_call x1, Pallas kernels: 79.4 us -> 80.7 us  [local_step(): pl.pallas_call(kernel, out_shape=(vm((TOK, D), BF),) + got + (vm((2, 32,...]
where the time goes in v7:
time: 83.3 us; the launch traced here: 83.2 us
  Pallas kernels  82.4 us (99%)
  between operations  0.84 us (1%)
    pallas_call x1, Pallas kernels, local_step(): pl.pallas_call(kernel, out_shape=(vm((TOK, D), BF),) + got + (vm((2, 32,...  80.7 us
    pallas_call x1, Pallas kernels, local_step(): pl.pallas_call(finish, out_shape=(sds(TOK, D),) + grads + grads, in_specs...  1.69 us

profile of v7, /device:TPU:0, one launch (start us, length us, event | category | flops | bytes accessed | tf_op | source)
XLA Modules:
  0.0 83.2 jit_solution(1720661560092653578)
XLA Ops:
  0.6 80.7 %moe_backward.1 = (bf16[512,256]{1,0:T(8,128)(2,1)S(1)}, bf16[2,2,128,896]{3,2,1,0:T(8,128)(2,1)S(1)}, bf16[2,2,128,896]{3,2,1,0:T(8,128)(2,1)S(1)}, bf16[2,2,89...) custom-call(bf16[512,256]{1,0:T(8,128)(2,1)} %tokens.1, bf16[512,256]{1,0:T(8,128)(2,1)} %dy.1, s32[2,512]{1,0:T(2,128)} %bitcast.4, ...), custom_call_target="tpu_custom_call" | custom-call | tf_op jit(solution)/shard_map/moe_backward/pallas_call | solution.py:513
  81.3 1.7 %finish.1 = (bf16[512,256]{1,0:T(8,128)(2,1)}, bf16[32,256]{1,0:T(8,128)(2,1)}, bf16[2,128,896]{2,1,0:T(8,128)(2,1)}, bf16[2,128,896]{2,1,0:T(8,128)(2,1)}, bf16...) custom-call(bf16[512,256]{1,0:T(8,128)(2,1)S(1)} %get-tuple-element., ...), custom_call_target="tpu_custom_call" | custom-call | tf_op jit(solution)/shard_map/finish/pallas_call | solution.py:523
